TPU v7x, 32 devices: a whole 2x2x4 slice. The times are simulated.
32 devices in a mesh: dom: 16 (over z, x, core), rep: 2 (over y).
Axes of the slice: x: 2, y: 2, z: 4, core: 2. Of those that a mesh axis runs over, the one named last changes fastest.
Arguments:
- features: bfloat16 [131072, 128], P('dom'), may hold values from -6 to 6
- partition_map: int32 [131072], replicated, may hold values from 0 to 131071, as said below
- seed_ids: int32 [2048], P(('dom', 'rep')), may hold values from 0 to 131071, as said below
- hop1_ids: int32 [2048, 15], P(('dom', 'rep')), may hold values from 0 to 131071, as said below
- hop2_ids: int32 [2048, 15, 10], P(('dom', 'rep')), may hold values from 0 to 131071, as said below
- labels: int32 [2048], P(('dom', 'rep')), may hold values from 0 to 171
- self_one: bfloat16 [128, 256], replicated, may hold values from -0.5 to 0.5
- neigh_one: bfloat16 [128, 256], replicated, may hold values from -0.5 to 0.5
- bias_one: float32 [256], replicated, may hold values from -3 to 3
- self_two: bfloat16 [256, 172], replicated, may hold values from -0.375 to 0.375
- neigh_two: bfloat16 [256, 172], replicated, may hold values from -0.375 to 0.375
- bias_two: float32 [172], replicated, may hold values from -2 to 112, as said below
Outputs:
- seed_loss: float32 [2048], P(('dom', 'rep'))
- grad_self_one: float32 [128, 256], replicated
- grad_neigh_one: float32 [128, 256], replicated
- grad_bias_one: float32 [256], replicated
- grad_self_two: float32 [256, 172], replicated
- grad_neigh_two: float32 [256, 172], replicated
- grad_bias_two: float32 [172], replicated
Inputs may be any that keep to these rules, and one draw needn't show every extreme that they name: A permutation of 0 to 131071: node v is stored at position p = partition_map[v], in partition p // 8192, row p % 8192. Rows below 256 of each partition hold hub nodes. `seed_ids`: node ids. `hop1_ids`: node ids. `hop2_ids`: take one device's 64 seeds (an aligned block of seeds) with all their hop-1 and hop-2 ids, 10624 ids with repeats counted, and map them through partition_map: at most 2428 positions fall in any one partition, and at most 332 fall in rows 256 and above of any one partition. Every device reaches both bounds. `bias_two`: class biases.
All inputs are finite; a program needn't handle non-finite values.
Results may differ from a plain program's by a relative error of at most 0.003.
Values may be sent and summed in bfloat16 or wider, within the bound.
A program may use at most 128 MiB of HBM per device.

v0:
```python
import jax
import jax.numpy as jnp
from jax import lax
from jax.sharding import PartitionSpec as P

HOT_DEV = 256


def activate(values):
    return jax.nn.gelu(values, approximate=True)


def sage_terms(
    seed_rows,
    hop_rows,
    far_rows,
    labels,
    self_one,
    neigh_one,
    bias_one,
    self_two,
    neigh_two,
    bias_two,
):
    seed_count = seed_rows.shape[0]
    fan_one = hop_rows.shape[0] // seed_count
    feat_width = seed_rows.shape[1]
    hidden = self_one.shape[1]
    seed_mean = jnp.mean(
        hop_rows.reshape(seed_count, fan_one, feat_width), axis=1, dtype=jnp.float32
    ).astype(jnp.bfloat16)
    far_mean = jnp.mean(far_rows, axis=1, dtype=jnp.float32).astype(jnp.bfloat16)
    pre_seed = (
        jnp.dot(seed_rows, self_one, preferred_element_type=jnp.float32)
        + jnp.dot(seed_mean, neigh_one, preferred_element_type=jnp.float32)
        + bias_one
    )
    pre_hop = (
        jnp.dot(hop_rows, self_one, preferred_element_type=jnp.float32)
        + jnp.dot(far_mean, neigh_one, preferred_element_type=jnp.float32)
        + bias_one
    )
    act_seed, back_seed = jax.vjp(activate, pre_seed)
    act_hop, back_hop = jax.vjp(activate, pre_hop)
    hid_seed = act_seed.astype(jnp.bfloat16)
    hid_hop = act_hop.astype(jnp.bfloat16)
    hop_mean = jnp.mean(
        hid_hop.reshape(seed_count, fan_one, hidden), axis=1, dtype=jnp.float32
    ).astype(jnp.bfloat16)
    logits = (
        jnp.dot(hid_seed, self_two, preferred_element_type=jnp.float32)
        + jnp.dot(hop_mean, neigh_two, preferred_element_type=jnp.float32)
        + bias_two
    )
    peak_value = jnp.max(logits, axis=1, keepdims=True)
    shifted = logits - peak_value
    log_total = jnp.log(jnp.sum(jnp.exp(shifted), axis=1, keepdims=True))
    log_probs = shifted - log_total
    class_iota = lax.broadcasted_iota(jnp.int32, logits.shape, 1)
    target = (labels[:, None] == class_iota).astype(jnp.float32)
    seed_loss = -jnp.sum(log_probs * target, axis=1)
    d_logits = ((jnp.exp(log_probs) - target) / seed_count).astype(jnp.bfloat16)
    grad_self_two = jnp.dot(hid_seed.T, d_logits, preferred_element_type=jnp.float32)
    grad_neigh_two = jnp.dot(hop_mean.T, d_logits, preferred_element_type=jnp.float32)
    grad_bias_two = jnp.sum(d_logits.astype(jnp.float32), axis=0)
    d_hid_seed = jnp.dot(d_logits, self_two.T, preferred_element_type=jnp.float32)
    d_hop_mean = jnp.dot(d_logits, neigh_two.T, preferred_element_type=jnp.float32)
    d_pre_seed = back_seed(d_hid_seed)[0].astype(jnp.bfloat16)
    spread = jnp.broadcast_to(
        (d_hop_mean / fan_one)[:, None, :], (seed_count, fan_one, hidden)
    ).reshape(seed_count * fan_one, hidden)
    d_pre_hop = back_hop(spread)[0].astype(jnp.bfloat16)
    grad_self_one = jnp.dot(seed_rows.T, d_pre_seed, preferred_element_type=jnp.float32) + jnp.dot(
        hop_rows.T, d_pre_hop, preferred_element_type=jnp.float32
    )
    grad_neigh_one = jnp.dot(seed_mean.T, d_pre_seed, preferred_element_type=jnp.float32) + jnp.dot(
        far_mean.T, d_pre_hop, preferred_element_type=jnp.float32
    )
    grad_bias_one = jnp.sum(d_pre_seed.astype(jnp.float32), axis=0) + jnp.sum(
        d_pre_hop.astype(jnp.float32), axis=0
    )
    return (
        seed_loss,
        (
            grad_self_one,
            grad_neigh_one,
            grad_bias_one,
            grad_self_two,
            grad_neigh_two,
            grad_bias_two,
        ),
    )


def bucket_slots(owners, chosen, part_count):
    columns = lax.broadcasted_iota(jnp.int32, (owners.shape[0], part_count), 1)
    member = ((owners[:, None] == columns) & chosen[:, None]).astype(jnp.int32)
    running = jnp.cumsum(member, axis=0)
    return jnp.sum(running * member, axis=1) - 1


def request_table(owners, slots, local_rows, part_count, capacity):
    target_slot = jnp.where(slots >= 0, slots, capacity)
    table = jnp.zeros((part_count, capacity), jnp.int32)
    return table.at[owners, target_slot].set(local_rows, mode="drop")


def shards(
    features,
    partition_map,
    seed_ids,
    hop1_ids,
    hop2_ids,
    labels,
    self_one,
    neigh_one,
    bias_one,
    self_two,
    neigh_two,
    bias_two,
):
    part_count = lax.axis_size("dom")
    seed_count = seed_ids.shape[0]
    fan_one = hop1_ids.shape[1]
    fan_two = hop2_ids.shape[2]
    node_rows = features.shape[0]
    feat_width = features.shape[1]
    tree_rows = 1 + fan_one + fan_one * fan_two
    seed_unit = seed_count // part_count
    cold_cap = tree_rows // 2 * seed_unit
    wanted = jnp.concatenate([seed_ids, hop1_ids.reshape(-1), hop2_ids.reshape(-1)])
    position = partition_map[wanted]
    owners = position // node_rows
    local_rows = position % node_rows
    is_cold = local_rows >= HOT_DEV
    slots = bucket_slots(owners, is_cold, part_count)
    request = request_table(owners, slots, local_rows, part_count, cold_cap)
    arrived = lax.all_to_all(request, "dom", split_axis=0, concat_axis=0, tiled=True)
    returned = lax.all_to_all(features[arrived], "dom", split_axis=0, concat_axis=0, tiled=True)
    hub_rows = lax.all_gather(features[:HOT_DEV], "dom", axis=0, tiled=True)
    from_far = returned[owners, jnp.maximum(slots, 0)]
    from_hub = hub_rows[owners * HOT_DEV + jnp.minimum(local_rows, HOT_DEV - 1)]
    fetched = jnp.where(is_cold[:, None], from_far, from_hub)
    seed_rows = fetched[:seed_count]
    hop_rows = fetched[seed_count : seed_count * (1 + fan_one)]
    far_rows = fetched[seed_count * (1 + fan_one) :].reshape(
        seed_count * fan_one, fan_two, feat_width
    )
    seed_loss, grads = sage_terms(
        seed_rows,
        hop_rows,
        far_rows,
        labels,
        self_one,
        neigh_one,
        bias_one,
        self_two,
        neigh_two,
        bias_two,
    )
    grad_self_one, grad_neigh_one, grad_bias_one, grad_self_two, grad_neigh_two, grad_bias_two = (
        grads
    )
    summed = lax.psum(
        (
            grad_self_one,
            grad_neigh_one,
            grad_bias_one,
            grad_self_two,
            grad_neigh_two,
            grad_bias_two,
        ),
        ("dom", "rep"),
    )
    return (seed_loss, summed[0], summed[1], summed[2], summed[3], summed[4], summed[5])


def solution(mesh):
    return jax.shard_map(
        shards,
        mesh=mesh,
        in_specs=(
            P("dom", None),
            P(),
            P(("dom", "rep")),
            P(("dom", "rep"), None),
            P(("dom", "rep"), None, None),
            P(("dom", "rep")),
            P(),
            P(),
            P(),
            P(),
            P(),
            P(),
        ),
        out_specs=(P(("dom", "rep")), P(), P(), P(), P(), P(), P()),
        check_vma=False,
    )
```

profile of v0, /device:TPU:0, one launch (start us, length us, event | category | flops | bytes accessed | tf_op | source)
XLA Modules:
  0.0 499.6 jit_solution(7547511234379188678)
XLA Ops:
  7.2 1.2 copy.25
  8.4 0.3 concatenate.36
  8.7 0.8 copy.24
  9.5 0.1 concatenate.35
  9.7 0.8 concatenate.37
  10.4 0.1 fusion.30
  10.6 54.9 %gather_fusion = s32[10624]{0:T(1024)S(1)} fusion(s32[131072]{0:T(1024)S(1)} %copy-done, s32[11264]{0:T(1024)S(1)} %pad_clamp_fusion.1), kind=kCustom, calls=%fused_computation | custom fusion | bytes 127488 | tf_op jit(solution)/shard_map/gather | solution.py:132
  65.6 0.9 fusion.11
  66.6 9.2 %reduce-window.6 = s32[16,83,128]{2,1,0:T(8,128)S(1)} reduce-window(s32[16,83,128]{2,1,0:T(8,128)} %fusion.11, s32[]{:T(128)} %constant.33.clone.1), window={size=1x1x128 pad=0_0x0_0x127_0}, to_apply=%region_0.1 | reduce-window | flops 21587968 | bytes 1359876 | tf_op jit(solution)/shard_map/reduce-window
  75.8 0.6 slice_reduce_fusion
  76.3 0.2 reduce-window.9
  76.6 0.3 broadcast_add_fusion
  76.8 0.3 fusion.13
  77.1 0.8 or_reduce_fusion
  77.9 0.2 multiply_reduce_fusion
  78.1 0.2 and_reduce_fusion
  78.3 50.0 %scatter_custom_fusion = s32[5312]{0:T(1024)S(1)} fusion(s32[10624]{0:T(1024)S(1)} %broadcast_select_fusion.1, s32[10624]{0:T(1024)S(1)} %get-tuple-element.22, s32[]{:T(128)} %constant.33.clone.1), kind=kCustom, calls=%fused_computation.111 | custom fusion | bytes 21252
  128.3 0.1 all_to_all.11
  128.4 13.8 %all_to_all.17 = s32[16,1,332]{2,1,0:T(1,128)S(1)} all-to-all(s32[16,1,332]{2,1,0:T(1,128)S(1)} %all_to_all.11), channel_id=1, replica_groups=mesh['dom'=16,'rep'=2] {'dom'}, dimensions={0} | all-to-all | bytes 42496 | tf_op jit(solution)/shard_map/all_to_all | solution.py:138
  142.3 0.1 reshape.365
  142.4 11.6 %gather_fusion.1 = bf16[5312,128]{1,0:T(8,128)(2,1)} fusion(bf16[8192,128]{1,0:T(8,128)(2,1)S(1)} %copy-done.1, s32[6144]{0:T(1024)S(1)} %pad_clamp_fusion.2), kind=kCustom, calls=%fused_computation.1 | custom fusion | bytes 2740992 | tf_op jit(solution)/shard_map/gather | solution.py:139
  154.1 2.3 reshape.364
  156.4 4.4 all-to-all-start.1
  160.8 0.6 slice.20
  161.5 0.2 all-reduce.4.cloned.1.call-start
  161.7 46.3 %all-gather.2.cloned.1.call-done = bf16[4096,128]{1,0:T(8,128)(2,1)} async-done(((bf16[256,128]{1,0:T(8,128)(2,1)}), bf16[4096,128]{1,0:T(8,128)(2,1)}) %all-gather.2.cloned.1.call-update) | async-done | bytes 1048592 | tf_op jit(solution)/shard_map/all_gather | solution.py:140
  208.1 21.8 %gather_fusion.3 = bf16[10624,128]{1,0:T(8,128)(2,1)} fusion(bf16[4096,128]{1,0:T(8,128)(2,1)} %all-gather.2.cloned.1.call-done, s32[11264]{0:T(1024)S(1)} %pad_clamp_fusion), kind=kCustom, calls=%fused_computation.3 | custom fusion | bytes 5481984 | tf_op jit(solution)/shard_map/gather | solution.py:142
  229.9 1.7 copy.26
  231.6 76.5 %gather_fusion.2 = bf16[10624,128]{1,0:T(8,128)(2,1)} fusion(bf16[16,332,128]{2,0,1:T(8,128)(2,1)S(1)} %copy.26, s32[10624]{0:T(1024)S(1)} %get-tuple-element.19), kind=kCustom, calls=%fused_computation.2 | custom fusion | bytes 5524480 | tf_op jit(solution)/shard_map/gather | solution.py:141
  308.1 7.6 %broadcast_select_fusion = bf16[10624,128]{1,0:T(8,128)(2,1)S(1)} fusion(bf16[10624,128]{1,0:T(8,128)(2,1)} %gather_fusion.2, bf16[10624,128]{1,0:T(8,128)(2,1)} %gather_fusion.3, pred[10624]{0:T(1024)(128)(4,1)S(1)} %get-tuple-element.21), kind=kLoop, calls=%fused_computation.5 | loop fusion | flops 1359872 | bytes 8169856 | tf_op jit(solution)/shard_map/jit(_where)/select_n | solution.py:143
  315.7 2.4 slice_convert_fusion
  318.1 0.8 slice_convert_fusion.1
  318.9 1.3 fusion.17
  320.2 0.8 fusion.39
  320.9 6.6 %reshape.353 = f32[960,10,128]{2,1,0:T(8,128)} reshape(f32[9600,128]{1,0:T(8,128)} %slice_convert_fusion) | data formatting | bytes 9830400 | tf_op jit(solution)/shard_map/convert_element_type | solution.py:32
  327.6 5.3 %reduce_sum.83 = f32[960,128]{1,0:T(8,128)} reduce(f32[960,10,128]{2,1,0:T(8,128)} %reshape.353, f32[]{:T(128)} %constant.78.clone.1), dimensions={1}, to_apply=%region_5.6 | reduce | flops 1105920 | bytes 5406724 | tf_op jit(solution)/shard_map/reduce_sum | solution.py:32
  332.9 3.2 fusion.15
  336.1 2.3 reshape.354
  338.4 1.4 reduce_sum.84
  339.8 1.9 reshape.352
  341.7 1.1 reduce_sum.82
  342.8 1.0 fusion.2
  343.8 1.1 fusion.52
  344.9 0.3 fusion.55
  345.1 0.2 exponential_reduce_fusion
  345.4 0.2 convert_reduce_fusion.1
  345.6 0.1 convolution_multiply_fusion
  345.7 1.1 convert_reduce_fusion.2
  346.8 0.9 fusion.41
  347.7 0.9 fusion.51
  348.6 0.2 fusion.44
  348.8 0.2 fusion.37
  349.0 1.1 broadcast_in_dim.13
  350.1 2.3 reshape.346
  352.4 2.3 convert_reduce_fusion
  354.6 0.9 convolution_add_fusion.1
  355.5 0.9 convolution_add_fusion.2
  356.5 0.5 neg.3
  357.0 38.9 %all-reduce = (f32[256]{0:T(256)}, f32[172]{0:T(256)}) all-reduce(f32[256]{0:T(256)S(1)} %add.216, f32[172]{0:T(256)S(1)} %get-tuple-element.13), channel_id=1, replica_groups=mesh['dom'=16,'rep'=2] {'dom','rep'}, use_global_device_ids=true, to_apply=%region_14.15 | all-reduce | flops 428 | bytes 3424 | tf_op jit(solution)/shard_map/psum | solution.py:164
  395.9 90.5 %all-reduce.4.cloned.1.call-done = (f32[128,256]{1,0:T(8,128)}, f32[128,256]{1,0:T(8,128)}, f32[256,172]{0,1:T(8,128)}, f32[256,172]{0,1:T(8,128)}) async-done(((f32[128,256]{1,0:T(8,128)}, f32[128,256]{1,0:T(8,128)}, f32[256,172]{0,1:T(8,128)}, f32[256,172]{0,1:T(8,128)}), (f32[128,256]{1,0:T(8,128)}, f32[128,256]{1,0:T(8,128)}, f32[256,172]{0,1:T(8,128)}, ...) | async-done | bytes 614416 | tf_op jit(solution)/shard_map/psum | solution.py:164
  486.4 1.6 copy.33
  488.0 1.6 copy.34
  489.5 1.6 copy.35
  491.1 1.6 copy.36
  (38 shorter events, 0.4 us)
Async XLA Ops:
  7.2 3.4 copy-start
  65.6 12.3 %copy-start.10 = (s32[2]{0:T(128)S(1)}, s32[2]{0:T(128)}, u32[]{:S(2)}) copy-start(s32[2]{0:T(128)} %constant.89) | copy-start | bytes 28
  65.6 12.5 %copy-start.9 = (s32[2]{0:T(128)S(1)}, s32[2]{0:T(128)}, u32[]{:S(2)}) copy-start(s32[2]{0:T(128)} %constant.92) | copy-start | bytes 28
  66.6 75.8 %copy-start.1 = (bf16[8192,128]{1,0:T(8,128)(2,1)S(1)}, bf16[8192,128]{1,0:T(8,128)(2,1)}, u32[]{:S(2)}) copy-start(bf16[8192,128]{1,0:T(8,128)(2,1)} %param.12) | copy-start | bytes 6291460
  156.4 73.5 %all-to-all-start.1 = ((bf16[16,332,128]{2,1,0:T(8,128)(2,1)}), bf16[16,332,128]{2,1,0:T(8,128)(2,1)}, u32[]{:S(2)}, u32[]{:S(2)}) async-start(bf16[16,332,128]{2,1,0:T(8,128)(2,1)} %reshape.364), calls=%async_computation.1 | async-start | bytes 2752512 | tf_op jit(solution)/shard_map/all_to_all | solution.py:139
  160.8 47.3 %all-gather.2.cloned.1.call-start = ((), (), s32[]{:S(2)}) async-start(), calls=%async_computation.2 | async-start | bytes 1114112 | tf_op jit(solution)/shard_map/all_gather | solution.py:140
  161.5 324.9 %all-reduce.4.cloned.1.call-start = ((), (), s32[]{:S(2)}) async-start(), calls=%async_computation.3 | async-start | bytes 1245184 | tf_op jit(solution)/shard_map/psum | solution.py:164
  315.7 3.2 copy-start.5
  327.6 5.3 %copy-start.4 = (bf16[128,256]{1,0:T(8,128)(2,1)S(1)}, bf16[128,256]{1,0:T(8,128)(2,1)}, u32[]{:S(2)}) copy-start(bf16[128,256]{1,0:T(8,128)(2,1)} %param.19) | copy-start | bytes 196612
  327.6 5.3 %copy-start.6 = (f32[256]{0:T(256)S(1)}, f32[256]{0:T(256)}, u32[]{:S(2)}) copy-start(f32[256]{0:T(256)} %param.20) | copy-start | bytes 3076
  336.1 8.8 %copy-start.3 = (bf16[256,172]{0,1:T(8,128)(2,1)S(1)}, bf16[256,172]{0,1:T(8,128)(2,1)}, u32[]{:S(2)}) copy-start(bf16[256,172]{0,1:T(8,128)(2,1)} %param.22) | copy-start | bytes 264196
  336.1 8.8 %copy-start.7 = (f32[172]{0:T(256)S(1)}, f32[172]{0:T(256)}, u32[]{:S(2)}) copy-start(f32[172]{0:T(256)} %param.23) | copy-start | bytes 2068
  336.1 9.3 %copy-start.8 = (s32[64]{0:T(128)S(1)}, s32[64]{0:T(128)}, u32[]{:S(2)}) copy-start(s32[64]{0:T(128)} %param.17) | copy-start | bytes 772
  352.3 2.3 copy-start.2
Sparse Core Ops, SparseCore 0:
  164.3 43.7 all-gather.1
  356.6 129.7 all-reduce.3
where the time goes:
time: 501 us; the launch traced here: 500 us
  local copies, waits for them, and re-layouts  244 us (49%)
  waiting for transfers between devices  137 us (27%)
  blocking collectives  52.7 us (11%)
  other arithmetic  34.2 us (7%)
  between operations  14.3 us (3%)
  matrix products  12.8 us (3%)
    psum x1, waiting for transfers between devices, shards(): lax.psum((grad_self_one, grad_neigh_one, grad_bias_one, grad_self_two, gr...  90.5 us
    gather x1, local copies, waits for them, and re-layouts, shards(): from_far = returned[owners, jnp.maximum(slots, 0)]  76.5 us
    unnamed x29, local copies, waits for them, and re-layouts  58.4 us
    gather x1, local copies, waits for them, and re-layouts, shards(): position = partition_map[wanted]  54.9 us
    all_gather x1, waiting for transfers between devices, shards(): hub_rows = lax.all_gather(features[:HOT_DEV], 'dom', axis=0, tiled=True)  46.3 us
    psum x1, blocking collectives, shards(): lax.psum((grad_self_one, grad_neigh_one, grad_bias_one, grad_self_two, gr...  38.9 us
    gather x1, local copies, waits for them, and re-layouts, shards(): from_hub = hub_rows[owners * HOT_DEV + jnp.minimum(local_rows, HOT_DEV - 1)]  21.8 us
    gather x2, local copies, waits for them, and re-layouts, shards(): features[arrived]  13.9 us
  transfers between devices with their start and end apart: 3, of which 2 were waited for; matrix products, arithmetic and copies ran while one was open for 5% of the time, Pallas kernels for 0%

commit v1 on v0

v1 whole, which is shorter than its diff:
```python
import functools

import jax
import jax.numpy as jnp
from jax import lax
from jax.experimental import pallas as pl
from jax.experimental.pallas import tpu as pltpu
from jax.sharding import PartitionSpec as P

HOT_DEV = 256
LANES = 128
MESH = pl.DeviceIdType.MESH
VMEM_LIMIT = 56 * 1024 * 1024


def round_up(value, unit):
    return -(-value // unit) * unit


def dot_tn(left, right):
    return lax.dot_general(left, right, (((0,), (0,)), ((), ())), preferred_element_type=jnp.float32)


def dot_nt(left, right):
    return lax.dot_general(left, right, (((1,), (1,)), ((), ())), preferred_element_type=jnp.float32)


def dot_nn(left, right):
    return jnp.dot(left, right, preferred_element_type=jnp.float32)


def plan_kernel(ids_ref, map_ref, req_ref, addr_ref, own_ref, slot_ref, val_ref, *, parts, shift, stride, id_rows, cap_pad):
    rows = ids_ref.shape[0]
    blocks = rows // 8
    tiles = [ids_ref[8 * v : 8 * v + 8, :] for v in range(blocks)]
    high = [tile >> 7 for tile in tiles]
    low = [tile & (LANES - 1) for tile in tiles]

    def lookup(step, found):
        base = pl.multiple_of(step * 8, 8)
        block = map_ref[pl.ds(base, 8), :]
        found = list(found)
        for k in range(8):
            row = jnp.broadcast_to(block[k : k + 1, :], (8, LANES))
            for v in range(blocks):
                got = jnp.take_along_axis(row, low[v], axis=1, mode="promise_in_bounds")
                found[v] = jnp.where(high[v] == base + k, got, found[v])
        return tuple(found)

    zero = jnp.zeros((8, LANES), jnp.int32)
    found = lax.fori_loop(0, map_ref.shape[0] // 8, lookup, (zero,) * blocks)
    position = jnp.concatenate(found, axis=0)
    owner = position >> shift
    local = position & ((1 << shift) - 1)
    row_iota = lax.broadcasted_iota(jnp.int32, (rows, LANES), 0)
    is_cold = (local >= HOT_DEV) & (row_iota < id_rows)
    owner_cold = jnp.where(is_cold, owner, -1)
    upper = (
        lax.broadcasted_iota(jnp.int32, (LANES, LANES), 0) <= lax.broadcasted_iota(jnp.int32, (LANES, LANES), 1)
    ).astype(jnp.bfloat16)
    ones = jnp.ones((LANES, LANES), jnp.bfloat16)
    below = (
        lax.broadcasted_iota(jnp.int32, (rows, rows), 1) < lax.broadcasted_iota(jnp.int32, (rows, rows), 0)
    ).astype(jnp.bfloat16)
    slot = jnp.full((rows, LANES), -1.0, jnp.float32)
    for part in range(parts):
        hit = owner_cold == part
        member = hit.astype(jnp.bfloat16)
        ahead = dot_nn(below, member).astype(jnp.bfloat16)
        running = dot_nn(member, upper) + dot_nn(ahead, ones)
        slot = jnp.where(hit, running - 1.0, slot)
    slot = slot.astype(jnp.int32)
    addr_ref[...] = owner * stride + jnp.where(is_cold, HOT_DEV + slot, local)
    own_ref[...] = owner_cold
    slot_ref[...] = slot
    val_ref[...] = local
    part_iota = lax.broadcasted_iota(jnp.int32, (parts, LANES), 0)
    slot_iota = lax.broadcasted_iota(jnp.int32, (cap_pad, LANES), 0)

    def place(step, table):
        base = pl.multiple_of(step * 8, 8)
        own8 = own_ref[pl.ds(base, 8), :]
        slot8 = slot_ref[pl.ds(base, 8), :]
        val8 = val_ref[pl.ds(base, 8), :]
        for k in range(0, 8, 2):
            lefts, rights = [], []
            for q in range(k, k + 2):
                val = val8[q : q + 1, :].astype(jnp.float32)
                top = jnp.floor(val * (1.0 / LANES))
                mine = part_iota == own8[q : q + 1, :]
                lefts.append(
                    jnp.concatenate(
                        [jnp.where(mine, top, 0.0), jnp.where(mine, val - top * LANES, 0.0)], axis=0
                    ).astype(jnp.bfloat16)
                )
                rights.append((slot_iota == slot8[q : q + 1, :]).astype(jnp.bfloat16))
            table = table + dot_nt(jnp.concatenate(lefts, axis=1), jnp.concatenate(rights, axis=1))
        return table

    table = lax.fori_loop(0, blocks, place, jnp.zeros((2 * parts, cap_pad), jnp.float32))
    req_ref[...] = (table[:parts] * LANES + table[parts:]).astype(jnp.int32)


def plan(ids, partition_map, parts, node_rows, stride, id_rows, cap_pad):
    rows = ids.shape[0]
    kernel = functools.partial(
        plan_kernel,
        parts=parts,
        shift=node_rows.bit_length() - 1,
        stride=stride,
        id_rows=id_rows,
        cap_pad=cap_pad,
    )
    return pl.pallas_call(
        kernel,
        name="plan",
        out_shape=(
            jax.ShapeDtypeStruct((parts, cap_pad), jnp.int32),
            jax.ShapeDtypeStruct((rows, LANES), jnp.int32),
        ),
        in_specs=[pl.BlockSpec(memory_space=pltpu.VMEM)] * 2,
        out_specs=(pl.BlockSpec(memory_space=pltpu.VMEM),) * 2,
        scratch_shapes=[pltpu.VMEM((rows, LANES), jnp.int32)] * 3,
        compiler_params=pltpu.CompilerParams(vmem_limit_bytes=VMEM_LIMIT),
        cost_estimate=pl.CostEstimate(flops=40_000_000, bytes_accessed=1_000_000, transcendentals=0),
    )(ids, partition_map.reshape(-1, LANES))


ROOT = 0.7978845608028654
CUBE = 0.044715


def gelu_pair(pre):
    square = pre * pre
    bend = jnp.tanh(ROOT * pre * (1.0 + CUBE * square))
    half = 0.5 * (1.0 + bend)
    slope = half + 0.5 * pre * (1.0 - bend * bend) * (ROOT * (1.0 + 3.0 * CUBE * square))
    return pre * half, slope


def tree_sum(values):
    while len(values) > 1:
        values = [a + b for a, b in zip(values[::2], values[1::2])] + (
            [values[-1]] if len(values) % 2 else []
        )
    return values[0]


def model_kernel(
    addr_ref, table_ref, label_ref, w_one_ref, b_one_ref, w_two_ref, b_two_ref,
    loss_ref, g_one_ref, gb_one_ref, g_two_ref, gb_two_ref,
    wide, x_buf, far_buf, own_buf, slope_buf, d_buf, *, seeds, fan_one, fan_two,
):
    feat = table_ref.shape[1]
    hidden = w_one_ref.shape[1]
    hops = seeds * fan_one
    chunk = 64 if table_ref.shape[0] % 64 == 0 else 16

    def widen(step, carry):
        at = pl.ds(pl.multiple_of(step * chunk, chunk), chunk)
        wide[at, :] = table_ref[at, :].astype(jnp.float32)
        return carry

    lax.fori_loop(0, table_ref.shape[0] // chunk, widen, 0)

    def fetch(step, carry):
        j = step // (seeds // 8)
        block = step % (seeds // 8)
        base = pl.multiple_of(step * 8, 8)
        for k in range(8):
            hop = (block * 8 + k) * fan_one + j
            own_buf[pl.ds(base + k, 1), :] = wide[pl.ds(addr_ref[seeds + hop], 1), :]
            first = seeds + hops + hop * fan_two
            rows = [wide[pl.ds(addr_ref[first + m], 1), :] for m in range(fan_two)]
            far_buf[pl.ds(base + k, 1), :] = tree_sum(rows)
        return carry

    lax.fori_loop(0, hops // 8, fetch, 0)

    def fetch_seed(step, carry):
        base = pl.multiple_of(step * 8, 8)
        for k in range(8):
            own_buf[pl.ds(hops + base + k, 1), :] = wide[pl.ds(addr_ref[base + k], 1), :]
        return carry

    lax.fori_loop(0, seeds // 8, fetch_seed, 0)

    w_one = w_one_ref[...]
    b_one = b_one_ref[...]
    row_sum = jnp.zeros((seeds, feat), jnp.float32)
    hid_sum = jnp.zeros((seeds, hidden), jnp.float32)
    for j in range(fan_one):
        at = slice(j * seeds, (j + 1) * seeds)
        own = own_buf[at, :]
        row_sum = row_sum + own
        x_buf[at, :feat] = own.astype(jnp.bfloat16)
        x_buf[at, feat:] = (far_buf[at, :] * (1.0 / fan_two)).astype(jnp.bfloat16)
    x_buf[hops:, :feat] = own_buf[hops:, :].astype(jnp.bfloat16)
    x_buf[hops:, feat:] = (row_sum * (1.0 / fan_one)).astype(jnp.bfloat16)
    act = None
    for j in range(fan_one + 1):
        at = slice(j * seeds, (j + 1) * seeds)
        act, slope = gelu_pair(dot_nn(x_buf[at, :], w_one) + b_one)
        act = act.astype(jnp.bfloat16)
        slope_buf[at, :] = slope
        if j < fan_one:
            hid_sum = hid_sum + act.astype(jnp.float32)
    hid = jnp.concatenate([act, (hid_sum * (1.0 / fan_one)).astype(jnp.bfloat16)], axis=1)
    logits = dot_nn(hid, w_two_ref[...]) + b_two_ref[...]
    shifted = logits - jnp.max(logits, axis=1, keepdims=True)
    log_probs = shifted - jnp.log(jnp.sum(jnp.exp(shifted), axis=1, keepdims=True))
    class_iota = lax.broadcasted_iota(jnp.int32, logits.shape, 1)
    target = (class_iota == label_ref[...]).astype(jnp.float32)
    loss_ref[...] = -jnp.sum(log_probs * target, axis=1, keepdims=True)
    d_logits = ((jnp.exp(log_probs) - target) * (1.0 / seeds)).astype(jnp.bfloat16)
    g_two_ref[...] = dot_tn(hid, d_logits)
    gb_two_ref[...] = jnp.sum(d_logits.astype(jnp.float32), axis=0, keepdims=True)
    d_hid = dot_nt(d_logits, w_two_ref[...])
    d_hop = d_hid[:, hidden:] * (1.0 / fan_one)
    bias_sum = jnp.zeros((seeds, hidden), jnp.float32)
    for j in range(fan_one + 1):
        at = slice(j * seeds, (j + 1) * seeds)
        d_pre = ((d_hop if j < fan_one else d_hid[:, :hidden]) * slope_buf[at, :]).astype(jnp.bfloat16)
        d_buf[at, :] = d_pre
        bias_sum = bias_sum + d_pre.astype(jnp.float32)
    gb_one_ref[...] = jnp.sum(bias_sum, axis=0, keepdims=True)
    g_one_ref[...] = dot_tn(x_buf[...], d_buf[...])


def model(addr, table, labels, self_one, neigh_one, bias_one, self_two, neigh_two, bias_two, fan_one, fan_two):
    seeds = labels.shape[0]
    feat, hidden = self_one.shape
    classes = self_two.shape[1]
    total = seeds * (1 + fan_one)
    vmem = pl.BlockSpec(memory_space=pltpu.VMEM)
    return pl.pallas_call(
        functools.partial(model_kernel, seeds=seeds, fan_one=fan_one, fan_two=fan_two),
        name="model",
        out_shape=(
            jax.ShapeDtypeStruct((seeds, 1), jnp.float32),
            jax.ShapeDtypeStruct((2 * feat, hidden), jnp.float32),
            jax.ShapeDtypeStruct((1, hidden), jnp.float32),
            jax.ShapeDtypeStruct((2 * hidden, classes), jnp.float32),
            jax.ShapeDtypeStruct((1, classes), jnp.float32),
        ),
        in_specs=[pl.BlockSpec(memory_space=pltpu.SMEM)] + [vmem] * 6,
        out_specs=(vmem,) * 5,
        scratch_shapes=[
            pltpu.VMEM(table.shape, jnp.float32),
            pltpu.VMEM((total, 2 * feat), jnp.bfloat16),
            pltpu.VMEM((total - seeds, feat), jnp.float32),
            pltpu.VMEM((total, feat), jnp.float32),
            pltpu.VMEM((total, hidden), jnp.float32),
            pltpu.VMEM((total, hidden), jnp.bfloat16),
        ],
        compiler_params=pltpu.CompilerParams(vmem_limit_bytes=VMEM_LIMIT),
        cost_estimate=pl.CostEstimate(flops=100_000_000, bytes_accessed=4_000_000, transcendentals=0),
    )(
        addr,
        table,
        labels.reshape(seeds, 1),
        jnp.concatenate([self_one, neigh_one], axis=0),
        bias_one.reshape(1, hidden),
        jnp.concatenate([self_two, neigh_two], axis=0),
        bias_two.reshape(1, classes),
    )


def reduce_kernel(part_ref, out_ref, inbox, gathered, local_sem, send_sem, recv_sem, send_two, recv_two, *, n_dom, n_rep):
    count = n_dom * n_rep
    me = lax.axis_index("dom") * n_rep + lax.axis_index("rep")
    barrier = pltpu.get_barrier_semaphore()

    def peer(step):
        other = lax.rem(me + step, count)
        return other, {"dom": other // n_rep, "rep": lax.rem(other, n_rep)}

    def greet(step, carry):
        other, where = peer(step)
        pl.semaphore_signal(barrier, inc=1, device_id=where, device_id_type=MESH)
        return carry

    lax.fori_loop(1, count, greet, 0)
    keep = pltpu.make_async_copy(part_ref.at[me], inbox.at[me], local_sem)
    keep.start()
    pl.semaphore_wait(barrier, count - 1)

    def scatter(step, carry):
        other, where = peer(step)
        pltpu.make_async_remote_copy(
            part_ref.at[other], inbox.at[me], send_sem, recv_sem, device_id=where, device_id_type=MESH
        ).start()
        return carry

    lax.fori_loop(1, count, scatter, 0)
    keep.wait()
    most = pl.ds(0, count - 1)
    first = pltpu.make_async_remote_copy(
        part_ref.at[most], inbox.at[most], send_sem, recv_sem, device_id=peer(1)[1], device_id_type=MESH
    )
    first.wait_recv()
    total = inbox[0].astype(jnp.float32)

    def add(step, total):
        return total + inbox[step].astype(jnp.float32)

    total = lax.fori_loop(1, count, add, total)
    gathered[me] = total.astype(gathered.dtype)

    def spread(step, carry):
        other, where = peer(step)
        pltpu.make_async_remote_copy(
            gathered.at[me], gathered.at[me], send_two, recv_two, device_id=where, device_id_type=MESH
        ).start()
        return carry

    lax.fori_loop(1, count, spread, 0)
    second = pltpu.make_async_remote_copy(
        gathered.at[most], gathered.at[most], send_two, recv_two, device_id=peer(1)[1], device_id_type=MESH
    )
    second.wait_recv()
    first.wait_send()
    second.wait_send()
    out_ref[...] = gathered[...]


def sum_everywhere(pieces):
    n_dom, n_rep = lax.axis_size("dom"), lax.axis_size("rep")
    count = n_dom * n_rep
    vmem = pl.BlockSpec(memory_space=pltpu.VMEM)
    return pl.pallas_call(
        functools.partial(reduce_kernel, n_dom=n_dom, n_rep=n_rep),
        name="sum_everywhere",
        out_shape=jax.ShapeDtypeStruct(pieces.shape, pieces.dtype),
        in_specs=[vmem],
        out_specs=vmem,
        scratch_shapes=[
            pltpu.VMEM(pieces.shape, pieces.dtype),
            pltpu.VMEM(pieces.shape, pieces.dtype),
            pltpu.SemaphoreType.DMA,
            pltpu.SemaphoreType.DMA,
            pltpu.SemaphoreType.DMA,
            pltpu.SemaphoreType.DMA,
            pltpu.SemaphoreType.DMA,
        ],
        compiler_params=pltpu.CompilerParams(collective_id=1, has_side_effects=True, vmem_limit_bytes=VMEM_LIMIT),
    )(pieces)


def shards(
    features, partition_map, seed_ids, hop1_ids, hop2_ids, labels,
    self_one, neigh_one, bias_one, self_two, neigh_two, bias_two,
):
    parts = lax.axis_size("dom")
    count = parts * lax.axis_size("rep")
    seeds = seed_ids.shape[0]
    fan_one = hop1_ids.shape[1]
    fan_two = hop2_ids.shape[2]
    node_rows, feat = features.shape
    tree_rows = 1 + fan_one + fan_one * fan_two
    cold_cap = tree_rows // 2 * (seeds // parts)
    cap_row = round_up(cold_cap, 16)
    cap_pad = round_up(cold_cap, LANES)
    stride = HOT_DEV + cap_row
    total = seeds * tree_rows
    id_rows = total // LANES
    wanted = jnp.concatenate([seed_ids, hop1_ids.reshape(-1), hop2_ids.reshape(-1)])
    ids = jnp.pad(wanted.reshape(id_rows, LANES), ((0, round_up(id_rows, 8) - id_rows), (0, 0)))
    request, addr = plan(ids, partition_map, parts, node_rows, stride, id_rows, cap_pad)
    arrived = lax.all_to_all(request[:, :cap_row], "dom", split_axis=0, concat_axis=0, tiled=True)
    returned = lax.all_to_all(features[arrived], "dom", split_axis=0, concat_axis=0, tiled=True)
    hubs = lax.all_gather(features[:HOT_DEV], "dom", axis=0)
    table = jnp.concatenate([hubs, returned], axis=1).reshape(parts * stride, feat)
    loss, g_one, gb_one, g_two, gb_two = model(
        addr.reshape(-1), table, labels, self_one, neigh_one, bias_one, self_two, neigh_two, bias_two,
        fan_one, fan_two,
    )
    hidden, classes = self_two.shape
    sizes = [g_one.size, g_two.size, gb_one.size, gb_two.size]
    flat = jnp.concatenate([g_one.reshape(-1), g_two.reshape(-1), gb_one.reshape(-1), gb_two.reshape(-1)])
    rows = round_up(-(-flat.size // (count * LANES)), 8)
    flat = jnp.pad(flat, (0, count * rows * LANES - flat.size))
    summed = sum_everywhere(flat.reshape(count, rows, LANES)).reshape(-1)
    cuts = [0]
    for size in sizes:
        cuts.append(cuts[-1] + size)
    one = summed[cuts[0] : cuts[1]].reshape(2, feat, hidden)
    two = summed[cuts[1] : cuts[2]].reshape(2, hidden, classes)
    return (
        loss.reshape(-1), one[0], one[1], summed[cuts[2] : cuts[3]],
        two[0], two[1], summed[cuts[3] : cuts[4]],
    )


def solution(mesh):
    return jax.shard_map(
        shards,
        mesh=mesh,
        in_specs=(
            P("dom", None),
            P(),
            P(("dom", "rep")),
            P(("dom", "rep"), None),
            P(("dom", "rep"), None, None),
            P(("dom", "rep")),
            P(),
            P(),
            P(),
            P(),
            P(),
            P(),
        ),
        out_specs=(P(("dom", "rep")), P(), P(), P(), P(), P(), P()),
        check_vma=False,
    )
```

time: 501 us -> 209 us (0.42)
  the two profiles are of different devices: /device:TPU:0 before, /device:TPU:27 now
where the time goes in v1:
time: 209 us
  Pallas kernels  102 us (49%)
  waiting for transfers between devices  38.8 us (19%)
  local copies, waits for them, and re-layouts  30 us (14%)
  between operations  14.2 us (7%)
  blocking collectives  8.5 us (4%)
  starting transfers between devices  8 us (4%)
  other arithmetic  7.37 us (4%)
    pallas_call x1, Pallas kernels, plan(): pl.pallas_call(kernel, name='plan', out_shape=(jax.ShapeDtypeStruct((part...  47.2 us
    all_gather x1, waiting for transfers between devices, shards(): hubs = lax.all_gather(features[:HOT_DEV], 'dom', axis=0)  38.7 us
    pallas_call x1, Pallas kernels, sum_everywhere(): pl.pallas_call(functools.partial(reduce_kernel, n_dom=n_dom, n_rep=n_rep)...  38.2 us
    pallas_call x1, Pallas kernels, model(): pl.pallas_call(functools.partial(model_kernel, seeds=seeds, fan_one=fan_o...  16.4 us
    gather x1, local copies, waits for them, and re-layouts, shards(): features[arrived]  11.6 us
    all_to_all x1, blocking collectives, shards(): lax.all_to_all(request[:, :cap_row], 'dom', split_axis=0, concat_axis=0,...  8.5 us
    all_to_all x1, starting transfers between devices, shards(): lax.all_to_all(features[arrived], 'dom', split_axis=0, concat_axis=0, til...  7.96 us
    unnamed x15, local copies, waits for them, and re-layouts  6.77 us
  transfers between devices with their start and end apart: 2, of which 1 were waited for; matrix products, arithmetic and copies ran while one was open for 3% of the time, Pallas kernels for 0%

profile of v1, /device:TPU:27, one launch (start us, length us, event | category | flops | bytes accessed | tf_op | source)
XLA Modules:
  0.0 208.6 jit_solution(6623453160303216399)
XLA Ops:
  7.2 0.0 copy-start
  7.2 0.9 copy.29
  8.1 0.1 reshape.112
  8.2 1.2 copy.30
  9.4 0.3 reshape.113
  9.7 0.7 concatenate.15
  10.5 0.6 pad.8.ids_ref
  11.1 47.2 %plan.1 = (s32[16,384]{1,0:T(8,128)}, s32[88,128]{1,0:T(8,128)}) custom-call(s32[88,128]{1,0:T(8,128)} %pad.8.ids_ref, s32[1024,128]{1,0:T(8,128)} %bitcast.27), custom_call_target="tpu_custom_call" | custom-call | flops 40000000 | bytes 1000000 | tf_op jit(solution)/shard_map/plan/pallas_call | solution.py:114
  58.3 0.7 slice_bitcast_fusion
  59.1 8.5 %all_to_all.17 = s32[16,1,336]{2,1,0:T(1,128)S(1)} all-to-all(s32[16,1,336]{2,1,0:T(1,128)S(1)} %copy.31), channel_id=1, replica_groups=mesh['dom'=16,'rep'=2] {'dom'}, dimensions={0} | all-to-all | bytes 43008 | tf_op jit(solution)/shard_map/all_to_all | solution.py:370
  67.6 0.1 fusion
  67.7 0.1 reshape.130
  67.8 0.0 copy-done
  67.8 11.6 %gather_fusion = bf16[5376,128]{1,0:T(8,128)(2,1)} fusion(bf16[8192,128]{1,0:T(8,128)(2,1)S(1)} %copy-done, s32[6144]{0:T(1024)S(1)} %pad_clamp_fusion), kind=kCustom, calls=%fused_computation | custom fusion | bytes 2774016 | tf_op jit(solution)/shard_map/gather | solution.py:371
  79.4 0.0 copy-start.3
  79.4 0.0 copy-start.1
  79.4 8.0 %all-to-all-start.1 = ((bf16[16,336,128]{2,1,0:T(8,128)(2,1)}), bf16[16,336,128]{2,1,0:T(8,128)(2,1)S(1)}, u32[]{:S(2)}, u32[]{:S(2)}) async-start(bf16[16,336,128]{2,1,0:T(8,128)(2,1)} %bitcast.20), calls=%async_computation.1 | async-start | bytes 2752512 | tf_op jit(solution)/shard_map/all_to_all | solution.py:371
  87.4 0.0 all-gather.3.cloned.1.call-start
  87.5 0.6 slice.48
  88.1 0.0 all-gather.3.cloned.1.call-update
  88.1 0.0 copy-done.3
  88.2 0.7 copy.34.label_ref
  88.9 1.0 copy.33
  89.9 1.0 copy.32
  90.9 0.0 copy-done.1
  90.9 1.5 pad_maximum_fusion.2.w_one_ref
  92.4 0.8 pad_maximum_fusion.1.w_two_ref
  93.1 38.7 %all-gather.3.cloned.1.call-done = bf16[4096,128]{1,0:T(8,128)(2,1)} async-done(((bf16[256,128]{1,0:T(8,128)(2,1)}), bf16[4096,128]{1,0:T(8,128)(2,1)}) %all-gather.3.cloned.1.call-update) | async-done | bytes 1048592 | tf_op jit(solution)/shard_map/all_gather | solution.py:372
  131.8 0.0 all-to-all-done.1
  131.8 2.8 %pad_maximum_fusion = bf16[16,592,128]{2,1,0:T(8,128)(2,1)} fusion(bf16[16,336,128]{2,1,0:T(8,128)(2,1)S(1)} %all-to-all-done.1, bf16[16,256,128]{2,1,0:T(8,128)(2,1)} %bitcast.25), kind=kLoop, calls=%fused_computation.1 | loop fusion | flops 4849664 | bytes 4849664 | tf_op jit(solution)/shard_map/concatenate | solution.py:373
  134.7 16.4 %model.1 = (f32[64,1]{1,0:T(8,128)}, f32[256,256]{1,0:T(8,128)}, f32[1,256]{1,0:T(1,128)}, f32[512,172]{1,0:T(8,128)}, f32[1,172]{1,0:T(1,128)}) custom-call(s32[11264]{0:T(1024)} %bitcast.30, bf16[9472,128]{1,0:T(8,128)(2,1)} %bitcast.19, s32[64,1]{1,0:T(8,128)} %copy.34.label_ref, bf16[256,256]{1,0:T(8,128)(2,1)} %pad_maximum_fusion.2.w_one_ref, ...), custom_call_target="tpu_custom_call" | custom-call | flops 100000000 | bytes 4000000 | tf_op jit(solution)/shard_map/model/pallas_call | solution.py:236
  151.0 1.5 reshape.123
  152.5 1.1 copy.37
  153.6 1.6 select_maximum_fusion
  155.2 38.2 %sum_everywhere.1 = f32[32,40,128]{2,1,0:T(8,128)} custom-call(f32[32,40,128]{2,1,0:T(8,128)} %bitcast.24), custom_call_target="tpu_custom_call" | custom-call | tf_op jit(solution)/shard_map/sum_everywhere/pallas_call | solution.py:331
  193.4 0.0 copy-start.2
  193.4 1.3 slice.50
  194.7 1.2 slice.63
  195.9 1.0 fusion.1
  197.0 1.2 slice.66
  198.2 0.7 fusion.2
  198.9 0.3 slice.55
  199.2 0.8 copy.35
  200.0 0.3 slice.57
  200.4 0.8 copy.36
  201.2 0.0 copy-done.2
  201.2 0.6 reduce.1
  (2 shorter events, 0.0 us)
Async XLA Ops:
  7.2 60.6 %copy-start = (bf16[8192,128]{1,0:T(8,128)(2,1)S(1)}, bf16[8192,128]{1,0:T(8,128)(2,1)}, u32[]{:S(2)}) copy-start(bf16[8192,128]{1,0:T(8,128)(2,1)} %param.12) | copy-start | bytes 6291460
  79.4 8.7 %copy-start.3 = (s32[64]{0:T(128)S(1)}, s32[64]{0:T(128)}, u32[]{:S(2)}) copy-start(s32[64]{0:T(128)} %param.17) | copy-start | bytes 772
  79.4 11.4 %copy-start.1 = (bf16[128,256]{1,0:T(8,128)(2,1)S(1)}, bf16[128,256]{1,0:T(8,128)(2,1)}, u32[]{:S(2)}) copy-start(bf16[128,256]{1,0:T(8,128)(2,1)} %param.19) | copy-start | bytes 196612
  79.4 52.4 %all-to-all-start.1 = ((bf16[16,336,128]{2,1,0:T(8,128)(2,1)}), bf16[16,336,128]{2,1,0:T(8,128)(2,1)S(1)}, u32[]{:S(2)}, u32[]{:S(2)}) async-start(bf16[16,336,128]{2,1,0:T(8,128)(2,1)} %bitcast.20), calls=%async_computation.1 | async-start | bytes 2752512 | tf_op jit(solution)/shard_map/all_to_all | solution.py:371
  87.4 44.4 %all-gather.3.cloned.1.call-start = ((), (), s32[]{:S(2)}) async-start(), calls=%async_computation.2 | async-start | bytes 1114112 | tf_op jit(solution)/shard_map/all_gather | solution.py:372
  193.4 7.8 %copy-start.2 = (f32[64,1]{1,0:T(8,128)S(1)}, f32[64,1]{1,0:T(8,128)}, u32[]{:S(2)}) copy-start(f32[64,1]{1,0:T(8,128)} %get-tuple-element.16) | copy-start | bytes 772
Sparse Core Ops, SparseCore 0:
  91.0 40.8 all-gather.2

commit v2 on v1

--- a/solution.py
+++ b/solution.py
@@ -10,6 +10,7 @@
 HOT_DEV = 256
 LANES = 128
 MESH = pl.DeviceIdType.MESH
+WIRE = jnp.bfloat16
 VMEM_LIMIT = 56 * 1024 * 1024
 
 
@@ -29,27 +30,31 @@
     return jnp.dot(left, right, preferred_element_type=jnp.float32)
 
 
-def plan_kernel(ids_ref, map_ref, req_ref, addr_ref, own_ref, slot_ref, val_ref, *, parts, shift, stride, id_rows, cap_pad):
+def plan_kernel(ids_ref, map_ref, req_ref, addr_ref, own_ref, slot_ref, val_ref, pos_ref, *, parts, shift, stride, id_rows, cap_pad):
     rows = ids_ref.shape[0]
     blocks = rows // 8
-    tiles = [ids_ref[8 * v : 8 * v + 8, :] for v in range(blocks)]
-    high = [tile >> 7 for tile in tiles]
-    low = [tile & (LANES - 1) for tile in tiles]
-
-    def lookup(step, found):
+    stored = map_ref[...]
+    pieces = jnp.concatenate([stored >> 16, (stored >> 8) & 255, stored & 255], axis=1)
+    pieces = pieces.astype(jnp.float32).astype(jnp.bfloat16)
+    map_iota = lax.broadcasted_iota(jnp.int32, map_ref.shape, 0)
+    lane_iota = lax.broadcasted_iota(jnp.int32, (LANES, 2 * LANES), 0)
+
+    def lookup(step, carry):
         base = pl.multiple_of(step * 8, 8)
-        block = map_ref[pl.ds(base, 8), :]
-        found = list(found)
-        for k in range(8):
-            row = jnp.broadcast_to(block[k : k + 1, :], (8, LANES))
-            for v in range(blocks):
-                got = jnp.take_along_axis(row, low[v], axis=1, mode="promise_in_bounds")
-                found[v] = jnp.where(high[v] == base + k, got, found[v])
-        return tuple(found)
-
-    zero = jnp.zeros((8, LANES), jnp.int32)
-    found = lax.fori_loop(0, map_ref.shape[0] // 8, lookup, (zero,) * blocks)
-    position = jnp.concatenate(found, axis=0)
+        tile = ids_ref[pl.ds(base, 8), :]
+        high, low = tile >> 7, tile & (LANES - 1)
+        for k in range(0, 8, 2):
+            hot = [(map_iota == high[q : q + 1, :]).astype(jnp.bfloat16) for q in (k, k + 1)]
+            found = dot_tn(pieces, jnp.concatenate(hot, axis=1))
+            found = found[:LANES] * 65536.0 + found[LANES : 2 * LANES] * 256.0 + found[2 * LANES :]
+            lane = jnp.concatenate([low[k : k + 1, :], low[k + 1 : k + 2, :]], axis=1)
+            picked = jnp.sum(jnp.where(lane_iota == lane, found, 0.0), axis=0, keepdims=True)
+            pos_ref[pl.ds(base + k, 1), :] = picked[:, :LANES].astype(jnp.int32)
+            pos_ref[pl.ds(base + k + 1, 1), :] = picked[:, LANES:].astype(jnp.int32)
+        return carry
+
+    lax.fori_loop(0, blocks, lookup, 0)
+    position = pos_ref[...]
     owner = position >> shift
     local = position & ((1 << shift) - 1)
     row_iota = lax.broadcasted_iota(jnp.int32, (rows, LANES), 0)
@@ -98,7 +103,10 @@
         return table
 
     table = lax.fori_loop(0, blocks, place, jnp.zeros((2 * parts, cap_pad), jnp.float32))
-    req_ref[...] = (table[:parts] * LANES + table[parts:]).astype(jnp.int32)
+    request = (table[:parts] * LANES + table[parts:]).astype(jnp.int32)
+    req_ref[...] = jnp.zeros(req_ref.shape, jnp.int32)
+    for c in range(cap_pad // LANES):
+        req_ref[:, c, :] = request[:, c * LANES : (c + 1) * LANES]
 
 
 def plan(ids, partition_map, parts, node_rows, stride, id_rows, cap_pad):
@@ -115,12 +123,12 @@
         kernel,
         name="plan",
         out_shape=(
-            jax.ShapeDtypeStruct((parts, cap_pad), jnp.int32),
+            jax.ShapeDtypeStruct((parts, round_up(cap_pad // LANES, 8), LANES), jnp.int32),
             jax.ShapeDtypeStruct((rows, LANES), jnp.int32),
         ),
         in_specs=[pl.BlockSpec(memory_space=pltpu.VMEM)] * 2,
         out_specs=(pl.BlockSpec(memory_space=pltpu.VMEM),) * 2,
-        scratch_shapes=[pltpu.VMEM((rows, LANES), jnp.int32)] * 3,
+        scratch_shapes=[pltpu.VMEM((rows, LANES), jnp.int32)] * 4,
         compiler_params=pltpu.CompilerParams(vmem_limit_bytes=VMEM_LIMIT),
         cost_estimate=pl.CostEstimate(flops=40_000_000, bytes_accessed=1_000_000, transcendentals=0),
     )(ids, partition_map.reshape(-1, LANES))
@@ -148,7 +156,7 @@
 
 def model_kernel(
     addr_ref, table_ref, label_ref, w_one_ref, b_one_ref, w_two_ref, b_two_ref,
-    loss_ref, g_one_ref, gb_one_ref, g_two_ref, gb_two_ref,
+    loss_ref, pack_ref,
     wide, x_buf, far_buf, own_buf, slope_buf, d_buf, *, seeds, fan_one, fan_two,
 ):
     feat = table_ref.shape[1]
@@ -213,8 +221,8 @@
     target = (class_iota == label_ref[...]).astype(jnp.float32)
     loss_ref[...] = -jnp.sum(log_probs * target, axis=1, keepdims=True)
     d_logits = ((jnp.exp(log_probs) - target) * (1.0 / seeds)).astype(jnp.bfloat16)
-    g_two_ref[...] = dot_tn(hid, d_logits)
-    gb_two_ref[...] = jnp.sum(d_logits.astype(jnp.float32), axis=0, keepdims=True)
+    g_two = dot_tn(hid, d_logits)
+    gb_two = jnp.sum(d_logits.astype(jnp.float32), axis=0, keepdims=True)
     d_hid = dot_nt(d_logits, w_two_ref[...])
     d_hop = d_hid[:, hidden:] * (1.0 / fan_one)
     bias_sum = jnp.zeros((seeds, hidden), jnp.float32)
@@ -223,11 +231,11 @@
         d_pre = ((d_hop if j < fan_one else d_hid[:, :hidden]) * slope_buf[at, :]).astype(jnp.bfloat16)
         d_buf[at, :] = d_pre
         bias_sum = bias_sum + d_pre.astype(jnp.float32)
-    gb_one_ref[...] = jnp.sum(bias_sum, axis=0, keepdims=True)
-    g_one_ref[...] = dot_tn(x_buf[...], d_buf[...])
-
-
-def model(addr, table, labels, self_one, neigh_one, bias_one, self_two, neigh_two, bias_two, fan_one, fan_two):
+    gb_one = jnp.sum(bias_sum, axis=0, keepdims=True)
+    pack_gradients(pack_ref, dot_tn(x_buf[...], d_buf[...]), gb_one, g_two, gb_two)
+
+
+def model(addr, table, labels, self_one, neigh_one, bias_one, self_two, neigh_two, bias_two, fan_one, fan_two, pack_rows):
     seeds = labels.shape[0]
     feat, hidden = self_one.shape
     classes = self_two.shape[1]
@@ -238,13 +246,10 @@
         name="model",
         out_shape=(
             jax.ShapeDtypeStruct((seeds, 1), jnp.float32),
-            jax.ShapeDtypeStruct((2 * feat, hidden), jnp.float32),
-            jax.ShapeDtypeStruct((1, hidden), jnp.float32),
-            jax.ShapeDtypeStruct((2 * hidden, classes), jnp.float32),
-            jax.ShapeDtypeStruct((1, classes), jnp.float32),
+            jax.ShapeDtypeStruct((pack_rows, LANES), WIRE),
         ),
         in_specs=[pl.BlockSpec(memory_space=pltpu.SMEM)] + [vmem] * 6,
-        out_specs=(vmem,) * 5,
+        out_specs=(vmem,) * 2,
         scratch_shapes=[
             pltpu.VMEM(table.shape, jnp.float32),
             pltpu.VMEM((total, 2 * feat), jnp.bfloat16),
@@ -266,8 +271,157 @@
     )
 
 
-def reduce_kernel(part_ref, out_ref, inbox, gathered, local_sem, send_sem, recv_sem, send_two, recv_two, *, n_dom, n_rep):
+def exchange_kernel(
+    req_ref, feat_ref, out_ref, inbox, wanted, wide, stage, send,
+    local_sem, req_send, req_recv, hub_send, hub_recv, row_send, row_recv, *, parts,
+):
+    node_rows = feat_ref.shape[0]
+    cap_row = send.shape[1]
+    me = lax.axis_index("dom")
+    barrier = pltpu.get_barrier_semaphore()
+
+    def where(step):
+        other = lax.rem(me + step, parts)
+        return other, {"dom": other}
+
+    def greet(step, carry):
+        pl.semaphore_signal(barrier, inc=1, device_id=where(step)[1], device_id_type=MESH)
+        return carry
+
+    lax.fori_loop(1, parts, greet, 0)
+    keep_req = pltpu.make_async_copy(req_ref.at[me], inbox.at[me], local_sem.at[0])
+    keep_req.start()
+    keep_hub = pltpu.make_async_copy(feat_ref.at[pl.ds(0, HOT_DEV)], out_ref.at[me, pl.ds(0, HOT_DEV)], local_sem.at[1])
+    keep_hub.start()
+    pl.semaphore_wait(barrier, parts - 1)
+
+    def ask(step, carry):
+        other, at = where(step)
+        pltpu.make_async_remote_copy(
+            req_ref.at[other], inbox.at[me], req_send, req_recv, device_id=at, device_id_type=MESH
+        ).start()
+        return carry
+
+    def share(step, carry):
+        pltpu.make_async_remote_copy(
+            feat_ref.at[pl.ds(0, HOT_DEV)], out_ref.at[me, pl.ds(0, HOT_DEV)], hub_send, hub_recv,
+            device_id=where(step)[1], device_id_type=MESH,
+        ).start()
+        return carry
+
+    lax.fori_loop(1, parts, ask, 0)
+    lax.fori_loop(1, parts, share, 0)
+
+    def widen(step, carry):
+        at = pl.ds(pl.multiple_of(step * 64, 64), 64)
+        wide[at, :] = feat_ref[at, :].astype(jnp.float32)
+        return carry
+
+    lax.fori_loop(0, node_rows // 64, widen, 0)
+    most = pl.ds(0, parts - 1)
+    asked = pltpu.make_async_remote_copy(
+        req_ref.at[most], inbox.at[most], req_send, req_recv, device_id=where(1)[1], device_id_type=MESH
+    )
+    keep_req.wait()
+    asked.wait_recv()
+    to_scalar = pltpu.make_async_copy(inbox, wanted, local_sem.at[2])
+    to_scalar.start()
+    to_scalar.wait()
+
+    def collect(other):
+        def block(step, carry):
+            base = pl.multiple_of(step * 16, 16)
+            row = step // (LANES // 16)
+            lane = lax.rem(step, LANES // 16) * 16
+            for k in range(16):
+                stage[pl.ds(base + k, 1), :] = wide[pl.ds(wanted[other, row, lane + k], 1), :]
+            return carry
+
+        lax.fori_loop(0, cap_row // 16, block, 0)
+        return stage[...].astype(jnp.bfloat16)
+
+    rows_at = pl.ds(HOT_DEV, cap_row)
+
+    def serve(step, carry):
+        other, at = where(step)
+        send[other] = collect(other)
+        pltpu.make_async_remote_copy(
+            send.at[other], out_ref.at[me, rows_at], row_send, row_recv, device_id=at, device_id_type=MESH
+        ).start()
+        return carry
+
+    lax.fori_loop(1, parts, serve, 0)
+    out_ref[me, HOT_DEV:, :] = collect(me)
+    hubs = pltpu.make_async_remote_copy(
+        out_ref.at[most, pl.ds(0, HOT_DEV)], out_ref.at[most, pl.ds(0, HOT_DEV)], hub_send, hub_recv,
+        device_id=where(1)[1], device_id_type=MESH,
+    )
+    rows = pltpu.make_async_remote_copy(
+        send.at[most], out_ref.at[most, rows_at], row_send, row_recv, device_id=where(1)[1], device_id_type=MESH
+    )
+    keep_hub.wait()
+    asked.wait_send()
+    hubs.wait()
+    rows.wait()
+
+
+def exchange(request, features, cap_row):
+    parts = lax.axis_size("dom")
+    node_rows, feat = features.shape
+    vmem = pl.BlockSpec(memory_space=pltpu.VMEM)
+    return pl.pallas_call(
+        functools.partial(exchange_kernel, parts=parts),
+        name="exchange",
+        out_shape=jax.ShapeDtypeStruct((parts, HOT_DEV + cap_row, feat), features.dtype),
+        in_specs=[vmem, vmem],
+        out_specs=vmem,
+        scratch_shapes=[
+            pltpu.VMEM(request.shape, jnp.int32),
+            pltpu.SMEM(request.shape, jnp.int32),
+            pltpu.VMEM((node_rows, feat), jnp.float32),
+            pltpu.VMEM((cap_row, feat), jnp.float32),
+            pltpu.VMEM((parts, cap_row, feat), features.dtype),
+            pltpu.SemaphoreType.DMA((3,)),
+        ]
+        + [pltpu.SemaphoreType.DMA] * 6,
+        compiler_params=pltpu.CompilerParams(collective_id=2, has_side_effects=True, vmem_limit_bytes=VMEM_LIMIT),
+    )(request, features)
+
+
+def pack_plan(feat, hidden, classes):
+    halves = hidden // LANES
+    one = 2 * feat * halves
+    low = one + 2 * hidden
+    tail = low + hidden
+    return halves, one, low, tail, tail + 16
+
+
+def pack_gradients(pack_ref, g_one, gb_one, g_two, gb_two):
+    hidden, feat = g_one.shape[1], g_one.shape[0] // 2
+    classes = g_two.shape[1]
+    halves, one, low, tail, used = pack_plan(feat, hidden, classes)
+    kind = pack_ref.dtype
+    for h in range(halves):
+        pack_ref[h * 2 * feat : (h + 1) * 2 * feat, :] = g_one[:, h * LANES : (h + 1) * LANES].astype(kind)
+    pack_ref[one:low, :] = g_two[:, :LANES].astype(kind)
+    rest = classes - LANES
+    blank = jnp.zeros((hidden, LANES // 2 - rest), jnp.float32)
+    high = jnp.concatenate([g_two[:hidden, LANES:], blank, g_two[hidden:, LANES:], blank], axis=1)
+    pack_ref[low:tail, :] = high.astype(kind)
+    wide = jnp.concatenate([gb_two, jnp.zeros((1, 2 * LANES - classes), jnp.float32)], axis=1)
+    pieces = [gb_one[:, h * LANES : (h + 1) * LANES] for h in range(halves)]
+    pieces += [wide[:, :LANES], wide[:, LANES:], jnp.zeros((16 - halves - 2, LANES), jnp.float32)]
+    pack_ref[tail:used, :] = jnp.concatenate(pieces, axis=0).astype(kind)
+    if pack_ref.shape[0] > used:
+        pack_ref[used:, :] = jnp.zeros((pack_ref.shape[0] - used, LANES), kind)
+
+
+def reduce_kernel(
+    part_ref, self_one, neigh_one, bias_one, self_two, neigh_two, bias_two,
+    inbox, gathered, local_sem, send_sem, recv_sem, send_two, recv_two, *, n_dom, n_rep,
+):
     count = n_dom * n_rep
+    rows = part_ref.shape[0] // count
     me = lax.axis_index("dom") * n_rep + lax.axis_index("rep")
     barrier = pltpu.get_barrier_semaphore()
 
@@ -275,42 +429,43 @@
         other = lax.rem(me + step, count)
         return other, {"dom": other // n_rep, "rep": lax.rem(other, n_rep)}
 
+    def block(index):
+        return pl.ds(pl.multiple_of(index * rows, rows), rows)
+
     def greet(step, carry):
-        other, where = peer(step)
-        pl.semaphore_signal(barrier, inc=1, device_id=where, device_id_type=MESH)
+        pl.semaphore_signal(barrier, inc=1, device_id=peer(step)[1], device_id_type=MESH)
         return carry
 
     lax.fori_loop(1, count, greet, 0)
-    keep = pltpu.make_async_copy(part_ref.at[me], inbox.at[me], local_sem)
+    keep = pltpu.make_async_copy(part_ref.at[block(me)], inbox.at[block(me)], local_sem)
     keep.start()
     pl.semaphore_wait(barrier, count - 1)
 
     def scatter(step, carry):
         other, where = peer(step)
         pltpu.make_async_remote_copy(
-            part_ref.at[other], inbox.at[me], send_sem, recv_sem, device_id=where, device_id_type=MESH
+            part_ref.at[block(other)], inbox.at[block(me)], send_sem, recv_sem, device_id=where, device_id_type=MESH
         ).start()
         return carry
 
     lax.fori_loop(1, count, scatter, 0)
     keep.wait()
-    most = pl.ds(0, count - 1)
+    most = pl.ds(0, (count - 1) * rows)
     first = pltpu.make_async_remote_copy(
         part_ref.at[most], inbox.at[most], send_sem, recv_sem, device_id=peer(1)[1], device_id_type=MESH
     )
     first.wait_recv()
-    total = inbox[0].astype(jnp.float32)
 
     def add(step, total):
-        return total + inbox[step].astype(jnp.float32)
-
-    total = lax.fori_loop(1, count, add, total)
-    gathered[me] = total.astype(gathered.dtype)
+        return total + inbox[block(step), :].astype(jnp.float32)
+
+    total = lax.fori_loop(0, count, add, jnp.zeros((rows, LANES), jnp.float32))
+    gathered[block(me), :] = total.astype(gathered.dtype)
 
     def spread(step, carry):
-        other, where = peer(step)
         pltpu.make_async_remote_copy(
-            gathered.at[me], gathered.at[me], send_two, recv_two, device_id=where, device_id_type=MESH
+            gathered.at[block(me)], gathered.at[block(me)], send_two, recv_two,
+            device_id=peer(step)[1], device_id_type=MESH,
         ).start()
         return carry
 
@@ -321,28 +476,38 @@
     second.wait_recv()
     first.wait_send()
     second.wait_send()
-    out_ref[...] = gathered[...]
-
-
-def sum_everywhere(pieces):
+    feat, hidden = self_one.shape
+    classes = self_two.shape[1]
+    rest = classes - LANES
+    halves, one, low, tail, used = pack_plan(feat, hidden, classes)
+    for h in range(halves):
+        cols = slice(h * LANES, (h + 1) * LANES)
+        at = h * 2 * feat
+        self_one[:, cols] = gathered[at : at + feat, :].astype(jnp.float32)
+        neigh_one[:, cols] = gathered[at + feat : at + 2 * feat, :].astype(jnp.float32)
+    self_two[:, :LANES] = gathered[one : one + hidden, :].astype(jnp.float32)
+    neigh_two[:, :LANES] = gathered[one + hidden : low, :].astype(jnp.float32)
+    high = gathered[low:tail, :].astype(jnp.float32)
+    self_two[:, LANES:] = high[:, :rest]
+    neigh_two[:, LANES:] = high[:, LANES // 2 : LANES // 2 + rest]
+    last = gathered[tail:used, :].astype(jnp.float32)
+    for h in range(halves):
+        bias_one[:, h * LANES : (h + 1) * LANES] = last[h : h + 1, :]
+    bias_two[:, :LANES] = last[halves : halves + 1, :]
+    bias_two[:, LANES:] = last[halves + 1 : halves + 2, :rest]
+
+
+def sum_everywhere(pieces, feat, hidden, classes):
     n_dom, n_rep = lax.axis_size("dom"), lax.axis_size("rep")
-    count = n_dom * n_rep
     vmem = pl.BlockSpec(memory_space=pltpu.VMEM)
+    shapes = [(feat, hidden), (feat, hidden), (1, hidden), (hidden, classes), (hidden, classes), (1, classes)]
     return pl.pallas_call(
         functools.partial(reduce_kernel, n_dom=n_dom, n_rep=n_rep),
         name="sum_everywhere",
-        out_shape=jax.ShapeDtypeStruct(pieces.shape, pieces.dtype),
+        out_shape=tuple(jax.ShapeDtypeStruct(shape, jnp.float32) for shape in shapes),
         in_specs=[vmem],
-        out_specs=vmem,
-        scratch_shapes=[
-            pltpu.VMEM(pieces.shape, pieces.dtype),
-            pltpu.VMEM(pieces.shape, pieces.dtype),
-            pltpu.SemaphoreType.DMA,
-            pltpu.SemaphoreType.DMA,
-            pltpu.SemaphoreType.DMA,
-            pltpu.SemaphoreType.DMA,
-            pltpu.SemaphoreType.DMA,
-        ],
+        out_specs=(vmem,) * 6,
+        scratch_shapes=[pltpu.VMEM(pieces.shape, pieces.dtype)] * 2 + [pltpu.SemaphoreType.DMA] * 5,
         compiler_params=pltpu.CompilerParams(collective_id=1, has_side_effects=True, vmem_limit_bytes=VMEM_LIMIT),
     )(pieces)
 
@@ -367,28 +532,18 @@
     wanted = jnp.concatenate([seed_ids, hop1_ids.reshape(-1), hop2_ids.reshape(-1)])
     ids = jnp.pad(wanted.reshape(id_rows, LANES), ((0, round_up(id_rows, 8) - id_rows), (0, 0)))
     request, addr = plan(ids, partition_map, parts, node_rows, stride, id_rows, cap_pad)
-    arrived = lax.all_to_all(request[:, :cap_row], "dom", split_axis=0, concat_axis=0, tiled=True)
-    returned = lax.all_to_all(features[arrived], "dom", split_axis=0, concat_axis=0, tiled=True)
-    hubs = lax.all_gather(features[:HOT_DEV], "dom", axis=0)
-    table = jnp.concatenate([hubs, returned], axis=1).reshape(parts * stride, feat)
-    loss, g_one, gb_one, g_two, gb_two = model(
+    table = exchange(request, features, cap_row).reshape(parts * stride, feat)
+    hidden, classes = self_two.shape
+    used = pack_plan(feat, hidden, classes)[-1]
+    pack_rows = count * round_up(-(-used // count), 16)
+    loss, pieces = model(
         addr.reshape(-1), table, labels, self_one, neigh_one, bias_one, self_two, neigh_two, bias_two,
-        fan_one, fan_two,
-    )
-    hidden, classes = self_two.shape
-    sizes = [g_one.size, g_two.size, gb_one.size, gb_two.size]
-    flat = jnp.concatenate([g_one.reshape(-1), g_two.reshape(-1), gb_one.reshape(-1), gb_two.reshape(-1)])
-    rows = round_up(-(-flat.size // (count * LANES)), 8)
-    flat = jnp.pad(flat, (0, count * rows * LANES - flat.size))
-    summed = sum_everywhere(flat.reshape(count, rows, LANES)).reshape(-1)
-    cuts = [0]
-    for size in sizes:
-        cuts.append(cuts[-1] + size)
-    one = summed[cuts[0] : cuts[1]].reshape(2, feat, hidden)
-    two = summed[cuts[1] : cuts[2]].reshape(2, hidden, classes)
+        fan_one, fan_two, pack_rows,
+    )
+    grads = sum_everywhere(pieces, feat, hidden, classes)
     return (
-        loss.reshape(-1), one[0], one[1], summed[cuts[2] : cuts[3]],
-        two[0], two[1], summed[cuts[3] : cuts[4]],
+        loss.reshape(-1), grads[0], grads[1], grads[2].reshape(-1),
+        grads[3], grads[4], grads[5].reshape(-1),
     )
 
 

time: 209 us -> 149 us (0.71)
  the two profiles are of different devices: /device:TPU:27 before, /device:TPU:0 now
where the time goes in v2:
time: 149 us; the launch traced here: 148 us
  Pallas kernels  128 us (86%)
  local copies, waits for them, and re-layouts  15.5 us (10%)
  other arithmetic  3.67 us (2%)
    pallas_call x1, Pallas kernels, exchange(): pl.pallas_call(functools.partial(exchange_kernel, parts=parts), name='exc...  51.3 us
    pallas_call x1, Pallas kernels, sum_everywhere(): pl.pallas_call(functools.partial(reduce_kernel, n_dom=n_dom, n_rep=n_rep)...  41.1 us
    pallas_call x1, Pallas kernels, plan(): pl.pallas_call(kernel, name='plan', out_shape=(jax.ShapeDtypeStruct((part...  19.7 us
    pallas_call x1, Pallas kernels, model(): pl.pallas_call(functools.partial(model_kernel, seeds=seeds, fan_one=fan_o...  16.4 us
    unnamed x12, local copies, waits for them, and re-layouts  13 us

profile of v2, /device:TPU:0, one launch (start us, length us, event | category | flops | bytes accessed | tf_op | source)
XLA Modules:
  0.0 148.3 jit_solution(3361631644076353525)
XLA Ops:
  0.6 0.0 copy-start
  0.6 0.8 copy.24
  1.4 0.1 reshape.50
  1.6 1.3 copy.28.label_ref
  2.9 1.5 %pad_maximum_fusion.1.w_one_ref = bf16[256,256]{1,0:T(8,128)(2,1)} fusion(bf16[128,256]{1,0:T(8,128)(2,1)} %param.19, bf16[128,256]{1,0:T(8,128)(2,1)} %param.18), kind=kLoop, calls=%fused_computation.1 | loop fusion | flops 262144 | bytes 262144 | tf_op jit(solution)/shard_map/concatenate | solution.py:267
  4.4 1.0 copy.26
  5.4 1.0 copy.27
  6.4 0.7 pad_maximum_fusion.w_two_ref
  7.2 1.2 copy.25
  8.4 0.3 reshape.51
  8.7 0.0 copy-done
  8.7 0.1 concatenate.9
  8.8 0.6 pad.4.ids_ref
  9.4 19.7 %plan.1 = (s32[16,8,128]{2,1,0:T(8,128)}, s32[88,128]{1,0:T(8,128)}) custom-call(s32[88,128]{1,0:T(8,128)} %pad.4.ids_ref, s32[1024,128]{1,0:T(8,128)} %bitcast.10), custom_call_target="tpu_custom_call" | custom-call | flops 40000000 | bytes 1000000 | tf_op jit(solution)/shard_map/plan/pallas_call | solution.py:122
  29.1 51.3 %exchange.1 = bf16[16,592,128]{2,1,0:T(8,128)(2,1)} custom-call(s32[16,8,128]{2,1,0:T(8,128)} %get-tuple-element.18.req_ref, bf16[8192,128]{1,0:T(8,128)(2,1)} %feat_ref.1), custom_call_target="tpu_custom_call" | custom-call | tf_op jit(solution)/shard_map/exchange/pallas_call | solution.py:372
  80.4 16.4 %model.1 = (f32[64,1]{1,0:T(8,128)}, bf16[1536,128]{1,0:T(8,128)(2,1)}) custom-call(s32[11264]{0:T(1024)} %bitcast.12, bf16[9472,128]{1,0:T(8,128)(2,1)} %bitcast.9, s32[64,1]{1,0:T(8,128)} %copy.28.label_ref, bf16[256,256]{1,0:T(8,128)(2,1)} %pad_maximum_fusion.1.w_one_ref, f32[1,256]{1,0:T(1,128)} %bitcast.13, bf16[512,172]{1,0:T(8,128)(2,1)} %pad_maximum_fusion.w_two_ref, ...), custom_call_target="tpu_custom_call" | custom-call | flops 100000000 | bytes 4000000 | tf_op jit(solution)/shard_map/model/pallas_call | solution.py:244
  96.8 1.4 reduce
  98.2 41.1 %sum_everywhere.1 = (f32[128,256]{1,0:T(8,128)}, f32[128,256]{1,0:T(8,128)}, f32[1,256]{1,0:T(1,128)}, f32[256,172]{1,0:T(8,128)}, f32[256,172]{1,0:T(8,128)}, /*index=5*/f32[1,172]{1,0:T(1,128)}) custom-call(bf16[1536,128]{1,0:T(8,128)(2,1)} %get-tuple-element.20.part_ref), custom_call_target="tpu_custom_call" | custom-call | tf_op jit(solution)/shard_map/sum_everywhere/pallas_call | solution.py:504
  139.3 1.7 %copy.29 = f32[256,172]{0,1:T(8,128)} copy(f32[256,172]{1,0:T(8,128)} %get-tuple-element.38) | data formatting | bytes 352256
  141.0 1.7 %copy.30 = f32[256,172]{0,1:T(8,128)} copy(f32[256,172]{1,0:T(8,128)} %get-tuple-element.39) | data formatting | bytes 352256
  142.7 1.6 %copy.35 = f32[128,256]{1,0:T(8,128)} copy(f32[128,256]{1,0:T(8,128)} %get-tuple-element.49) | data formatting | bytes 262144
  144.3 1.6 %copy.36 = f32[128,256]{1,0:T(8,128)} copy(f32[128,256]{1,0:T(8,128)} %get-tuple-element.50) | data formatting | bytes 262144
  145.9 1.2 copy.37
  147.1 1.2 copy.38
Async XLA Ops:
  0.6 8.0 %copy-start = (s32[64]{0:T(128)S(1)}, s32[64]{0:T(128)}, u32[]{:S(2)}) copy-start(s32[64]{0:T(128)} %param.14) | copy-start | bytes 772

commit v3 on v2

--- a/solution.py
+++ b/solution.py
@@ -10,7 +10,6 @@
 HOT_DEV = 256
 LANES = 128
 MESH = pl.DeviceIdType.MESH
-WIRE = jnp.bfloat16
 VMEM_LIMIT = 56 * 1024 * 1024
 
 
@@ -155,12 +154,12 @@
 
 
 def model_kernel(
-    addr_ref, table_ref, label_ref, w_one_ref, b_one_ref, w_two_ref, b_two_ref,
+    addr_ref, table_ref, label_ref, self_one, neigh_one, b_one_ref, self_two, neigh_two, b_two_ref,
     loss_ref, pack_ref,
     wide, x_buf, far_buf, own_buf, slope_buf, d_buf, *, seeds, fan_one, fan_two,
 ):
     feat = table_ref.shape[1]
-    hidden = w_one_ref.shape[1]
+    hidden = self_one.shape[1]
     hops = seeds * fan_one
     chunk = 64 if table_ref.shape[0] % 64 == 0 else 16
 
@@ -193,7 +192,8 @@
 
     lax.fori_loop(0, seeds // 8, fetch_seed, 0)
 
-    w_one = w_one_ref[...]
+    w_one = jnp.concatenate([self_one[...], neigh_one[...]], axis=0)
+    w_two = jnp.concatenate([self_two[...], neigh_two[...]], axis=0)
     b_one = b_one_ref[...]
     row_sum = jnp.zeros((seeds, feat), jnp.float32)
     hid_sum = jnp.zeros((seeds, hidden), jnp.float32)
@@ -214,24 +214,24 @@
         if j < fan_one:
             hid_sum = hid_sum + act.astype(jnp.float32)
     hid = jnp.concatenate([act, (hid_sum * (1.0 / fan_one)).astype(jnp.bfloat16)], axis=1)
-    logits = dot_nn(hid, w_two_ref[...]) + b_two_ref[...]
+    logits = dot_nn(hid, w_two) + b_two_ref[...]
     shifted = logits - jnp.max(logits, axis=1, keepdims=True)
     log_probs = shifted - jnp.log(jnp.sum(jnp.exp(shifted), axis=1, keepdims=True))
     class_iota = lax.broadcasted_iota(jnp.int32, logits.shape, 1)
-    target = (class_iota == label_ref[...]).astype(jnp.float32)
+    diagonal = lax.broadcasted_iota(jnp.int32, (seeds, seeds), 0) == lax.broadcasted_iota(jnp.int32, (seeds, seeds), 1)
+    label = jnp.sum(jnp.where(diagonal, label_ref[...].astype(jnp.float32), 0.0), axis=1, keepdims=True)
+    target = (class_iota.astype(jnp.float32) == label).astype(jnp.float32)
     loss_ref[...] = -jnp.sum(log_probs * target, axis=1, keepdims=True)
     d_logits = ((jnp.exp(log_probs) - target) * (1.0 / seeds)).astype(jnp.bfloat16)
     g_two = dot_tn(hid, d_logits)
-    gb_two = jnp.sum(d_logits.astype(jnp.float32), axis=0, keepdims=True)
-    d_hid = dot_nt(d_logits, w_two_ref[...])
+    gb_two = dot_tn(d_logits, jnp.ones((seeds, LANES), jnp.bfloat16))
+    d_hid = dot_nt(d_logits, w_two)
     d_hop = d_hid[:, hidden:] * (1.0 / fan_one)
-    bias_sum = jnp.zeros((seeds, hidden), jnp.float32)
     for j in range(fan_one + 1):
         at = slice(j * seeds, (j + 1) * seeds)
         d_pre = ((d_hop if j < fan_one else d_hid[:, :hidden]) * slope_buf[at, :]).astype(jnp.bfloat16)
         d_buf[at, :] = d_pre
-        bias_sum = bias_sum + d_pre.astype(jnp.float32)
-    gb_one = jnp.sum(bias_sum, axis=0, keepdims=True)
+    gb_one = dot_tn(d_buf[...], jnp.ones((d_buf.shape[0], LANES), jnp.bfloat16))
     pack_gradients(pack_ref, dot_tn(x_buf[...], d_buf[...]), gb_one, g_two, gb_two)
 
 
@@ -246,9 +246,9 @@
         name="model",
         out_shape=(
             jax.ShapeDtypeStruct((seeds, 1), jnp.float32),
-            jax.ShapeDtypeStruct((pack_rows, LANES), WIRE),
+            jax.ShapeDtypeStruct((pack_rows, LANES), jnp.float32),
         ),
-        in_specs=[pl.BlockSpec(memory_space=pltpu.SMEM)] + [vmem] * 6,
+        in_specs=[pl.BlockSpec(memory_space=pltpu.SMEM)] + [vmem] * 8,
         out_specs=(vmem,) * 2,
         scratch_shapes=[
             pltpu.VMEM(table.shape, jnp.float32),
@@ -263,54 +263,76 @@
     )(
         addr,
         table,
-        labels.reshape(seeds, 1),
-        jnp.concatenate([self_one, neigh_one], axis=0),
+        labels.reshape(1, seeds),
+        self_one,
+        neigh_one,
         bias_one.reshape(1, hidden),
-        jnp.concatenate([self_two, neigh_two], axis=0),
+        self_two,
+        neigh_two,
         bias_two.reshape(1, classes),
     )
 
 
 def exchange_kernel(
     req_ref, feat_ref, out_ref, inbox, wanted, wide, stage, send,
-    local_sem, req_send, req_recv, hub_send, hub_recv, row_send, row_recv, *, parts,
+    local_sem, req_send, req_recv, hub_send, hub_recv, row_send, row_recv, *, parts, asks,
 ):
     node_rows = feat_ref.shape[0]
     cap_row = send.shape[1]
     me = lax.axis_index("dom")
+    bits = parts.bit_length() - 1
     barrier = pltpu.get_barrier_semaphore()
 
-    def where(step):
-        other = lax.rem(me + step, parts)
+    def partner(mask):
+        other = me ^ mask
         return other, {"dom": other}
 
     def greet(step, carry):
-        pl.semaphore_signal(barrier, inc=1, device_id=where(step)[1], device_id_type=MESH)
+        pl.semaphore_signal(barrier, inc=1, device_id=partner(step)[1], device_id_type=MESH)
         return carry
 
     lax.fori_loop(1, parts, greet, 0)
+    hub_at = pl.ds(0, HOT_DEV)
+    ask_at = pl.ds(0, asks)
     keep_req = pltpu.make_async_copy(req_ref.at[me], inbox.at[me], local_sem.at[0])
     keep_req.start()
-    keep_hub = pltpu.make_async_copy(feat_ref.at[pl.ds(0, HOT_DEV)], out_ref.at[me, pl.ds(0, HOT_DEV)], local_sem.at[1])
+    keep_hub = pltpu.make_async_copy(feat_ref.at[hub_at], out_ref.at[me, hub_at], local_sem.at[1])
     keep_hub.start()
     pl.semaphore_wait(barrier, parts - 1)
 
     def ask(step, carry):
-        other, at = where(step)
+        other, at = partner(parts - step)
         pltpu.make_async_remote_copy(
-            req_ref.at[other], inbox.at[me], req_send, req_recv, device_id=at, device_id_type=MESH
+            req_ref.at[other, ask_at], inbox.at[me, ask_at], req_send, req_recv, device_id=at, device_id_type=MESH
         ).start()
         return carry
 
-    def share(step, carry):
-        pltpu.make_async_remote_copy(
-            feat_ref.at[pl.ds(0, HOT_DEV)], out_ref.at[me, pl.ds(0, HOT_DEV)], hub_send, hub_recv,
-            device_id=where(step)[1], device_id_type=MESH,
-        ).start()
-        return carry
-
     lax.fori_loop(1, parts, ask, 0)
-    lax.fori_loop(1, parts, share, 0)
+    keep_hub.wait()
+
+    def held(level, index):
+        return me ^ (index * (parts >> level))
+
+    def share(level):
+        at = partner(parts >> (level + 1))[1]
+
+        def one(index, carry):
+            slot = held(level, index)
+            pltpu.make_async_remote_copy(
+                out_ref.at[slot, hub_at], out_ref.at[slot, hub_at], hub_send.at[level], hub_recv.at[level],
+                device_id=at, device_id_type=MESH,
+            ).start()
+            return carry
+
+        lax.fori_loop(0, 1 << level, one, 0)
+
+    def shared(level):
+        some = out_ref.at[pl.ds(0, 1 << level), hub_at]
+        return pltpu.make_async_remote_copy(
+            some, some, hub_send.at[level], hub_recv.at[level], device_id=partner(1)[1], device_id_type=MESH
+        )
+
+    share(0)
 
     def widen(step, carry):
         at = pl.ds(pl.multiple_of(step * 64, 64), 64)
@@ -320,11 +342,12 @@
     lax.fori_loop(0, node_rows // 64, widen, 0)
     most = pl.ds(0, parts - 1)
     asked = pltpu.make_async_remote_copy(
-        req_ref.at[most], inbox.at[most], req_send, req_recv, device_id=where(1)[1], device_id_type=MESH
+        req_ref.at[most, ask_at], inbox.at[most, ask_at], req_send, req_recv,
+        device_id=partner(1)[1], device_id_type=MESH,
     )
     keep_req.wait()
     asked.wait_recv()
-    to_scalar = pltpu.make_async_copy(inbox, wanted, local_sem.at[2])
+    to_scalar = pltpu.make_async_copy(inbox.at[:, ask_at], wanted, local_sem.at[2])
     to_scalar.start()
     to_scalar.wait()
 
@@ -343,171 +366,246 @@
     rows_at = pl.ds(HOT_DEV, cap_row)
 
     def serve(step, carry):
-        other, at = where(step)
+        other, at = partner(parts - step)
         send[other] = collect(other)
         pltpu.make_async_remote_copy(
             send.at[other], out_ref.at[me, rows_at], row_send, row_recv, device_id=at, device_id_type=MESH
         ).start()
         return carry
 
-    lax.fori_loop(1, parts, serve, 0)
+    served = 1
+    for level in range(1, bits):
+        until = parts * level // bits
+        lax.fori_loop(served, until, serve, 0)
+        served = until
+        shared(level - 1).wait_recv()
+        share(level)
+    lax.fori_loop(served, parts, serve, 0)
     out_ref[me, HOT_DEV:, :] = collect(me)
-    hubs = pltpu.make_async_remote_copy(
-        out_ref.at[most, pl.ds(0, HOT_DEV)], out_ref.at[most, pl.ds(0, HOT_DEV)], hub_send, hub_recv,
-        device_id=where(1)[1], device_id_type=MESH,
-    )
     rows = pltpu.make_async_remote_copy(
-        send.at[most], out_ref.at[most, rows_at], row_send, row_recv, device_id=where(1)[1], device_id_type=MESH
-    )
-    keep_hub.wait()
+        send.at[most], out_ref.at[most, rows_at], row_send, row_recv, device_id=partner(1)[1], device_id_type=MESH
+    )
     asked.wait_send()
-    hubs.wait()
+    shared(bits - 1).wait_recv()
+    for level in range(bits):
+        shared(level).wait_send()
     rows.wait()
 
 
-def exchange(request, features, cap_row):
+def exchange(request, features, cap_row, asks):
     parts = lax.axis_size("dom")
+    bits = parts.bit_length() - 1
     node_rows, feat = features.shape
     vmem = pl.BlockSpec(memory_space=pltpu.VMEM)
     return pl.pallas_call(
-        functools.partial(exchange_kernel, parts=parts),
+        functools.partial(exchange_kernel, parts=parts, asks=asks),
         name="exchange",
         out_shape=jax.ShapeDtypeStruct((parts, HOT_DEV + cap_row, feat), features.dtype),
         in_specs=[vmem, vmem],
         out_specs=vmem,
         scratch_shapes=[
             pltpu.VMEM(request.shape, jnp.int32),
-            pltpu.SMEM(request.shape, jnp.int32),
+            pltpu.SMEM((parts, asks, LANES), jnp.int32),
             pltpu.VMEM((node_rows, feat), jnp.float32),
             pltpu.VMEM((cap_row, feat), jnp.float32),
             pltpu.VMEM((parts, cap_row, feat), features.dtype),
             pltpu.SemaphoreType.DMA((3,)),
-        ]
-        + [pltpu.SemaphoreType.DMA] * 6,
+            pltpu.SemaphoreType.DMA,
+            pltpu.SemaphoreType.DMA,
+            pltpu.SemaphoreType.DMA((bits,)),
+            pltpu.SemaphoreType.DMA((bits,)),
+            pltpu.SemaphoreType.DMA,
+            pltpu.SemaphoreType.DMA,
+        ],
         compiler_params=pltpu.CompilerParams(collective_id=2, has_side_effects=True, vmem_limit_bytes=VMEM_LIMIT),
     )(request, features)
 
 
-def pack_plan(feat, hidden, classes):
+def pack_plan(feat, hidden):
     halves = hidden // LANES
     one = 2 * feat * halves
     low = one + 2 * hidden
-    tail = low + hidden
-    return halves, one, low, tail, tail + 16
+    return halves, one, low, low + hidden
 
 
 def pack_gradients(pack_ref, g_one, gb_one, g_two, gb_two):
     hidden, feat = g_one.shape[1], g_one.shape[0] // 2
     classes = g_two.shape[1]
-    halves, one, low, tail, used = pack_plan(feat, hidden, classes)
-    kind = pack_ref.dtype
+    halves, one, low, used = pack_plan(feat, hidden)
     for h in range(halves):
-        pack_ref[h * 2 * feat : (h + 1) * 2 * feat, :] = g_one[:, h * LANES : (h + 1) * LANES].astype(kind)
-    pack_ref[one:low, :] = g_two[:, :LANES].astype(kind)
+        pack_ref[h * 2 * feat : (h + 1) * 2 * feat, :] = g_one[:, h * LANES : (h + 1) * LANES]
+    pack_ref[one:low, :] = g_two[:, :LANES]
     rest = classes - LANES
-    blank = jnp.zeros((hidden, LANES // 2 - rest), jnp.float32)
-    high = jnp.concatenate([g_two[:hidden, LANES:], blank, g_two[hidden:, LANES:], blank], axis=1)
-    pack_ref[low:tail, :] = high.astype(kind)
-    wide = jnp.concatenate([gb_two, jnp.zeros((1, 2 * LANES - classes), jnp.float32)], axis=1)
-    pieces = [gb_one[:, h * LANES : (h + 1) * LANES] for h in range(halves)]
-    pieces += [wide[:, :LANES], wide[:, LANES:], jnp.zeros((16 - halves - 2, LANES), jnp.float32)]
-    pack_ref[tail:used, :] = jnp.concatenate(pieces, axis=0).astype(kind)
+    space = LANES // 2 - rest
+    second = jnp.concatenate([gb_two[:, :1], jnp.zeros((hidden - classes, 1), jnp.float32)], axis=0)
+    pack_ref[low:used, :] = jnp.concatenate(
+        [
+            g_two[:hidden, LANES:], gb_one[:, :1], second, jnp.zeros((hidden, space - 2), jnp.float32),
+            g_two[hidden:, LANES:], jnp.zeros((hidden, space), jnp.float32),
+        ],
+        axis=1,
+    )
     if pack_ref.shape[0] > used:
-        pack_ref[used:, :] = jnp.zeros((pack_ref.shape[0] - used, LANES), kind)
-
-
-def reduce_kernel(
-    part_ref, self_one, neigh_one, bias_one, self_two, neigh_two, bias_two,
-    inbox, gathered, local_sem, send_sem, recv_sem, send_two, recv_two, *, n_dom, n_rep,
-):
-    count = n_dom * n_rep
-    rows = part_ref.shape[0] // count
-    me = lax.axis_index("dom") * n_rep + lax.axis_index("rep")
-    barrier = pltpu.get_barrier_semaphore()
-
-    def peer(step):
-        other = lax.rem(me + step, count)
-        return other, {"dom": other // n_rep, "rep": lax.rem(other, n_rep)}
-
-    def block(index):
-        return pl.ds(pl.multiple_of(index * rows, rows), rows)
-
-    def greet(step, carry):
-        pl.semaphore_signal(barrier, inc=1, device_id=peer(step)[1], device_id_type=MESH)
-        return carry
-
-    lax.fori_loop(1, count, greet, 0)
-    keep = pltpu.make_async_copy(part_ref.at[block(me)], inbox.at[block(me)], local_sem)
-    keep.start()
-    pl.semaphore_wait(barrier, count - 1)
-
-    def scatter(step, carry):
-        other, where = peer(step)
-        pltpu.make_async_remote_copy(
-            part_ref.at[block(other)], inbox.at[block(me)], send_sem, recv_sem, device_id=where, device_id_type=MESH
-        ).start()
-        return carry
-
-    lax.fori_loop(1, count, scatter, 0)
-    keep.wait()
-    most = pl.ds(0, (count - 1) * rows)
-    first = pltpu.make_async_remote_copy(
-        part_ref.at[most], inbox.at[most], send_sem, recv_sem, device_id=peer(1)[1], device_id_type=MESH
-    )
-    first.wait_recv()
-
-    def add(step, total):
-        return total + inbox[block(step), :].astype(jnp.float32)
-
-    total = lax.fori_loop(0, count, add, jnp.zeros((rows, LANES), jnp.float32))
-    gathered[block(me), :] = total.astype(gathered.dtype)
-
-    def spread(step, carry):
-        pltpu.make_async_remote_copy(
-            gathered.at[block(me)], gathered.at[block(me)], send_two, recv_two,
-            device_id=peer(step)[1], device_id_type=MESH,
-        ).start()
-        return carry
-
-    lax.fori_loop(1, count, spread, 0)
-    second = pltpu.make_async_remote_copy(
-        gathered.at[most], gathered.at[most], send_two, recv_two, device_id=peer(1)[1], device_id_type=MESH
-    )
-    second.wait_recv()
-    first.wait_send()
-    second.wait_send()
+        pack_ref[used:, :] = jnp.zeros((pack_ref.shape[0] - used, LANES), jnp.float32)
+
+
+def unpack_kernel(pack_ref, self_one, neigh_one, bias_one, self_two, neigh_two, bias_two):
     feat, hidden = self_one.shape
     classes = self_two.shape[1]
     rest = classes - LANES
-    halves, one, low, tail, used = pack_plan(feat, hidden, classes)
+    halves, one, low, used = pack_plan(feat, hidden)
     for h in range(halves):
         cols = slice(h * LANES, (h + 1) * LANES)
         at = h * 2 * feat
-        self_one[:, cols] = gathered[at : at + feat, :].astype(jnp.float32)
-        neigh_one[:, cols] = gathered[at + feat : at + 2 * feat, :].astype(jnp.float32)
-    self_two[:, :LANES] = gathered[one : one + hidden, :].astype(jnp.float32)
-    neigh_two[:, :LANES] = gathered[one + hidden : low, :].astype(jnp.float32)
-    high = gathered[low:tail, :].astype(jnp.float32)
+        self_one[:, cols] = pack_ref[at : at + feat, :]
+        neigh_one[:, cols] = pack_ref[at + feat : at + 2 * feat, :]
+    self_two[:, :LANES] = pack_ref[one : one + hidden, :]
+    neigh_two[:, :LANES] = pack_ref[one + hidden : low, :]
+    high = pack_ref[low:used, :]
     self_two[:, LANES:] = high[:, :rest]
     neigh_two[:, LANES:] = high[:, LANES // 2 : LANES // 2 + rest]
-    last = gathered[tail:used, :].astype(jnp.float32)
-    for h in range(halves):
-        bias_one[:, h * LANES : (h + 1) * LANES] = last[h : h + 1, :]
-    bias_two[:, :LANES] = last[halves : halves + 1, :]
-    bias_two[:, LANES:] = last[halves + 1 : halves + 2, :rest]
-
-
-def sum_everywhere(pieces, feat, hidden, classes):
-    n_dom, n_rep = lax.axis_size("dom"), lax.axis_size("rep")
+    turned = high.T
+    bias_one[...] = turned[rest : rest + 1, :]
+    bias_two[...] = turned[rest + 1 : rest + 2, :classes]
+
+
+def unpack(packed, feat, hidden, classes):
     vmem = pl.BlockSpec(memory_space=pltpu.VMEM)
     shapes = [(feat, hidden), (feat, hidden), (1, hidden), (hidden, classes), (hidden, classes), (1, classes)]
     return pl.pallas_call(
-        functools.partial(reduce_kernel, n_dom=n_dom, n_rep=n_rep),
-        name="sum_everywhere",
+        unpack_kernel,
+        name="unpack",
         out_shape=tuple(jax.ShapeDtypeStruct(shape, jnp.float32) for shape in shapes),
         in_specs=[vmem],
         out_specs=(vmem,) * 6,
-        scratch_shapes=[pltpu.VMEM(pieces.shape, pieces.dtype)] * 2 + [pltpu.SemaphoreType.DMA] * 5,
+        compiler_params=pltpu.CompilerParams(vmem_limit_bytes=VMEM_LIMIT),
+    )(packed)
+
+
+def reduce_kernel(
+    part_ref, out_ref, near_box, middle, far_box, gathered, send_sem, recv_sem, *, n_dom, n_rep, near,
+):
+    count = n_dom * n_rep
+    far = count // near
+    rows = part_ref.shape[0] // count
+    span = far * rows
+    me = lax.axis_index("dom") * n_rep + lax.axis_index("rep")
+    here, there = lax.rem(me, near), me // near
+    barrier = pltpu.get_barrier_semaphore()
+
+    def place(index):
+        return {"dom": index // n_rep, "rep": lax.rem(index, n_rep)}
+
+    def near_peer(step):
+        other = lax.rem(here + step, near)
+        return other, place(there * near + other)
+
+    def far_peer(step):
+        other = lax.rem(there + step, far)
+        return other, place(other * near + here)
+
+    def wide_at(index):
+        return pl.ds(pl.multiple_of(index * span, 8), span)
+
+    def thin_at(index):
+        return pl.ds(pl.multiple_of(index * rows, 8), rows)
+
+    def greet_near(step, carry):
+        pl.semaphore_signal(barrier, inc=1, device_id=near_peer(step)[1], device_id_type=MESH)
+        return carry
+
+    def greet_far(step, carry):
+        pl.semaphore_signal(barrier, inc=1, device_id=far_peer(step)[1], device_id_type=MESH)
+        return carry
+
+    lax.fori_loop(1, near, greet_near, 0)
+    lax.fori_loop(1, far, greet_far, 0)
+    pl.semaphore_wait(barrier, near + far - 2)
+
+    def copy(source, target, stage, where):
+        return pltpu.make_async_remote_copy(
+            source, target, send_sem.at[stage], recv_sem.at[stage], device_id=where, device_id_type=MESH
+        )
+
+    def out_near(step, carry):
+        other, where = near_peer(step)
+        copy(part_ref.at[wide_at(other)], near_box.at[wide_at(here)], 0, where).start()
+        return carry
+
+    lax.fori_loop(1, near, out_near, 0)
+    some = pl.ds(0, (near - 1) * span)
+    first = copy(part_ref.at[some], near_box.at[some], 0, near_peer(1)[1])
+    first.wait_recv()
+
+    def add_near(step, total):
+        return total + near_box[wide_at(near_peer(step)[0]), :]
+
+    middle[...] = lax.fori_loop(1, near, add_near, part_ref[wide_at(here), :])
+
+    def out_far(step, carry):
+        other, where = far_peer(step)
+        copy(middle.at[thin_at(other)], far_box.at[thin_at(there)], 1, where).start()
+        return carry
+
+    lax.fori_loop(1, far, out_far, 0)
+    some = pl.ds(0, (far - 1) * rows)
+    second = copy(middle.at[some], far_box.at[some], 1, far_peer(1)[1])
+    second.wait_recv()
+
+    def add_far(step, total):
+        return total + far_box[thin_at(far_peer(step)[0]), :]
+
+    total = lax.fori_loop(1, far, add_far, middle[thin_at(there), :])
+    mine = here * far + there
+    gathered[mine] = total.astype(gathered.dtype)
+
+    def back_far(step, carry):
+        copy(gathered.at[mine], gathered.at[mine], 2, far_peer(step)[1]).start()
+        return carry
+
+    lax.fori_loop(1, far, back_far, 0)
+    some = gathered.at[pl.ds(0, far - 1)]
+    third = copy(some, some, 2, far_peer(1)[1])
+    third.wait_recv()
+    group = gathered.at[pl.ds(here * far, far)]
+
+    def back_near(step, carry):
+        copy(group, group, 3, near_peer(step)[1]).start()
+        return carry
+
+    lax.fori_loop(1, near, back_near, 0)
+    some = gathered.at[pl.ds(0, (near - 1) * far)]
+    fourth = copy(some, some, 3, near_peer(1)[1])
+    fourth.wait_recv()
+    first.wait_send()
+    second.wait_send()
+    third.wait_send()
+    fourth.wait_send()
+    for index in range(count):
+        out_ref[index * rows : (index + 1) * rows, :] = gathered[index].astype(jnp.float32)
+
+
+def sum_everywhere(pieces):
+    n_dom, n_rep = lax.axis_size("dom"), lax.axis_size("rep")
+    count = n_dom * n_rep
+    near = 8
+    far = count // near
+    rows = pieces.shape[0] // count
+    vmem = pl.BlockSpec(memory_space=pltpu.VMEM)
+    return pl.pallas_call(
+        functools.partial(reduce_kernel, n_dom=n_dom, n_rep=n_rep, near=near),
+        name="sum_everywhere",
+        out_shape=jax.ShapeDtypeStruct(pieces.shape, jnp.float32),
+        in_specs=[vmem],
+        out_specs=vmem,
+        scratch_shapes=[
+            pltpu.VMEM(pieces.shape, jnp.float32),
+            pltpu.VMEM((far * rows, LANES), jnp.float32),
+            pltpu.VMEM((far * rows, LANES), jnp.float32),
+            pltpu.VMEM((count, rows, LANES), jnp.bfloat16),
+            pltpu.SemaphoreType.DMA((4,)),
+            pltpu.SemaphoreType.DMA((4,)),
+        ],
         compiler_params=pltpu.CompilerParams(collective_id=1, has_side_effects=True, vmem_limit_bytes=VMEM_LIMIT),
     )(pieces)
 
@@ -532,15 +630,15 @@
     wanted = jnp.concatenate([seed_ids, hop1_ids.reshape(-1), hop2_ids.reshape(-1)])
     ids = jnp.pad(wanted.reshape(id_rows, LANES), ((0, round_up(id_rows, 8) - id_rows), (0, 0)))
     request, addr = plan(ids, partition_map, parts, node_rows, stride, id_rows, cap_pad)
-    table = exchange(request, features, cap_row).reshape(parts * stride, feat)
+    table = exchange(request, features, cap_row, cap_pad // LANES).reshape(parts * stride, feat)
     hidden, classes = self_two.shape
-    used = pack_plan(feat, hidden, classes)[-1]
-    pack_rows = count * round_up(-(-used // count), 16)
+    used = pack_plan(feat, hidden)[-1]
+    pack_rows = count * round_up(-(-used // count), 8)
     loss, pieces = model(
         addr.reshape(-1), table, labels, self_one, neigh_one, bias_one, self_two, neigh_two, bias_two,
         fan_one, fan_two, pack_rows,
     )
-    grads = sum_everywhere(pieces, feat, hidden, classes)
+    grads = unpack(sum_everywhere(pieces), feat, hidden, classes)
     return (
         loss.reshape(-1), grads[0], grads[1], grads[2].reshape(-1),
         grads[3], grads[4], grads[5].reshape(-1),

time: 149 us -> 123 us (0.83)
  Pallas kernels: 128 us -> 109 us
  local copies, waits for them, and re-layouts: 15.5 us -> 10.5 us
  other arithmetic: 3.67 us -> 1.38 us
    pallas_call x2 -> x3, Pallas kernels: 92.4 us -> 73 us  [the longest x1 47.6 us: exchange(): pl.pallas_call(functools.partial(exchange_kernel, parts=parts, asks=asks)...]
    unnamed x12 -> x6, local copies, waits for them, and re-layouts: 13 us -> 8.74 us
    concatenate x2 -> x0, other arithmetic: 2.28 us -> none  [the longest x1 1.53 us: model(): jnp.concatenate([self_one, neigh_one], axis=0)]
where the time goes in v3:
time: 123 us; the launch traced here: 122 us
  Pallas kernels  109 us (89%)
  local copies, waits for them, and re-layouts  10.5 us (9%)
  other arithmetic  1.38 us (1%)
    pallas_call x1, Pallas kernels, exchange(): pl.pallas_call(functools.partial(exchange_kernel, parts=parts, asks=asks)...  47.6 us
    pallas_call x1, Pallas kernels, sum_everywhere(): pl.pallas_call(functools.partial(reduce_kernel, n_dom=n_dom, n_rep=n_rep,...  23.3 us
    pallas_call x1, Pallas kernels, plan(): pl.pallas_call(kernel, name='plan', out_shape=(jax.ShapeDtypeStruct((part...  19.7 us
    pallas_call x1, Pallas kernels, model(): pl.pallas_call(functools.partial(model_kernel, seeds=seeds, fan_one=fan_o...  16.4 us
    unnamed x6, local copies, waits for them, and re-layouts  8.74 us

profile of v3, /device:TPU:0, one launch (start us, length us, event | category | flops | bytes accessed | tf_op | source)
XLA Modules:
  0.0 121.6 jit_solution(9557248233332588106)
XLA Ops:
  0.6 0.8 copy.23
  1.4 0.1 reshape.50
  1.6 1.7 %copy.25.self_two = bf16[256,172]{1,0:T(8,128)(2,1)} copy(bf16[256,172]{0,1:T(8,128)(2,1)} %param.21) | data formatting | bytes 176128 | tf_op args[9]
  3.2 1.6 %copy.26.neigh_two = bf16[256,172]{1,0:T(8,128)(2,1)} copy(bf16[256,172]{0,1:T(8,128)(2,1)} %param.22) | data formatting | bytes 176128 | tf_op args[10]
  4.9 1.2 copy.24
  6.1 0.3 reshape.51
  6.3 0.7 concatenate.3
  7.1 0.6 pad.4.ids_ref
  7.7 19.7 %plan.1 = (s32[16,8,128]{2,1,0:T(8,128)}, s32[88,128]{1,0:T(8,128)}) custom-call(s32[88,128]{1,0:T(8,128)} %pad.4.ids_ref, s32[1024,128]{1,0:T(8,128)} %bitcast.10), custom_call_target="tpu_custom_call" | custom-call | flops 40000000 | bytes 1000000 | tf_op jit(solution)/shard_map/plan/pallas_call | solution.py:121
  27.4 47.6 %exchange.1 = bf16[16,592,128]{2,1,0:T(8,128)(2,1)} custom-call(s32[16,8,128]{2,1,0:T(8,128)} %get-tuple-element.18.req_ref, bf16[8192,128]{1,0:T(8,128)(2,1)} %feat_ref.1), custom_call_target="tpu_custom_call" | custom-call | tf_op jit(solution)/shard_map/exchange/pallas_call | solution.py:400
  75.0 16.4 %model.1 = (f32[64,1]{1,0:T(8,128)}, f32[1280,128]{1,0:T(8,128)}) custom-call(s32[11264]{0:T(1024)} %bitcast.12, bf16[9472,128]{1,0:T(8,128)(2,1)} %bitcast.9, s32[1,64]{1,0:T(1,128)} %bitcast.15, bf16[128,256]{1,0:T(8,128)(2,1)} %self_one.1, bf16[128,256]{1,0:T(8,128)(2,1)} %neigh_one.1, f32[1,256]{1,0:T(1,128)} %bitcast.13, ...), custom_call_target="tpu_custom_call" | custom-call | flops 100000000 | bytes 4000000 | tf_op jit(solution)/shard_map/model/pallas_call | solution.py:244
  91.4 1.4 %reduce = f32[64]{0:T(128)} reduce(f32[64,1]{1,0:T(8,128)} %get-tuple-element.19, f32[]{:T(128)} %constant.4), dimensions={1}, to_apply=%get-tuple-element.19.reduce_sub_computation | reduce | bytes 516 | tf_op jit(solution)/shard_map/model/pallas_call | solution.py:244
  92.8 23.3 %sum_everywhere.1.pack_ref = f32[1280,128]{1,0:T(8,128)} custom-call(f32[1280,128]{1,0:T(8,128)} %get-tuple-element.20.part_ref), custom_call_target="tpu_custom_call" | custom-call | tf_op jit(solution)/shard_map/sum_everywhere/pallas_call | solution.py:595
  116.1 2.0 %unpack.1 = (f32[128,256]{1,0:T(8,128)}, f32[128,256]{1,0:T(8,128)}, f32[1,256]{1,0:T(1,128)}, f32[256,172]{1,0:T(8,128)}, f32[256,172]{1,0:T(8,128)}, /*index=5*/f32[1,172]{1,0:T(1,128)}) custom-call(f32[1280,128]{1,0:T(8,128)} %sum_everywhere.1.pack_ref), custom_call_target="tpu_custom_call" | custom-call | tf_op jit(solution)/shard_map/unpack/pallas_call | solution.py:475
  118.2 1.7 %copy.27 = f32[256,172]{0,1:T(8,128)} copy(f32[256,172]{1,0:T(8,128)} %get-tuple-element.38) | data formatting | bytes 352256
  119.9 1.7 %copy.28 = f32[256,172]{0,1:T(8,128)} copy(f32[256,172]{1,0:T(8,128)} %get-tuple-element.39) | data formatting | bytes 352256

commit v4 on v3

--- a/solution.py
+++ b/solution.py
@@ -29,12 +29,12 @@
     return jnp.dot(left, right, preferred_element_type=jnp.float32)
 
 
-def plan_kernel(ids_ref, map_ref, req_ref, addr_ref, own_ref, slot_ref, val_ref, pos_ref, *, parts, shift, stride, id_rows, cap_pad):
+def plan_kernel(ids_ref, map_ref, req_ref, addr_ref, own_ref, slot_ref, val_ref, pos_ref, pieces_ref, *, parts, shift, stride, id_rows, cap_pad):
     rows = ids_ref.shape[0]
     blocks = rows // 8
     stored = map_ref[...]
     pieces = jnp.concatenate([stored >> 16, (stored >> 8) & 255, stored & 255], axis=1)
-    pieces = pieces.astype(jnp.float32).astype(jnp.bfloat16)
+    pieces_ref[...] = pieces.astype(jnp.float32).T.astype(jnp.bfloat16)
     map_iota = lax.broadcasted_iota(jnp.int32, map_ref.shape, 0)
     lane_iota = lax.broadcasted_iota(jnp.int32, (LANES, 2 * LANES), 0)
 
@@ -44,7 +44,7 @@
         high, low = tile >> 7, tile & (LANES - 1)
         for k in range(0, 8, 2):
             hot = [(map_iota == high[q : q + 1, :]).astype(jnp.bfloat16) for q in (k, k + 1)]
-            found = dot_tn(pieces, jnp.concatenate(hot, axis=1))
+            found = dot_nn(pieces_ref[...], jnp.concatenate(hot, axis=1))
             found = found[:LANES] * 65536.0 + found[LANES : 2 * LANES] * 256.0 + found[2 * LANES :]
             lane = jnp.concatenate([low[k : k + 1, :], low[k + 1 : k + 2, :]], axis=1)
             picked = jnp.sum(jnp.where(lane_iota == lane, found, 0.0), axis=0, keepdims=True)
@@ -127,7 +127,8 @@
         ),
         in_specs=[pl.BlockSpec(memory_space=pltpu.VMEM)] * 2,
         out_specs=(pl.BlockSpec(memory_space=pltpu.VMEM),) * 2,
-        scratch_shapes=[pltpu.VMEM((rows, LANES), jnp.int32)] * 4,
+        scratch_shapes=[pltpu.VMEM((rows, LANES), jnp.int32)] * 4
+        + [pltpu.VMEM((3 * LANES, partition_map.size // LANES), jnp.bfloat16)],
         compiler_params=pltpu.CompilerParams(vmem_limit_bytes=VMEM_LIMIT),
         cost_estimate=pl.CostEstimate(flops=40_000_000, bytes_accessed=1_000_000, transcendentals=0),
     )(ids, partition_map.reshape(-1, LANES))
@@ -193,7 +194,7 @@
     lax.fori_loop(0, seeds // 8, fetch_seed, 0)
 
     w_one = jnp.concatenate([self_one[...], neigh_one[...]], axis=0)
-    w_two = jnp.concatenate([self_two[...], neigh_two[...]], axis=0)
+    w_two = jnp.concatenate([self_two[...], neigh_two[...]], axis=1)
     b_one = b_one_ref[...]
     row_sum = jnp.zeros((seeds, feat), jnp.float32)
     hid_sum = jnp.zeros((seeds, hidden), jnp.float32)
@@ -214,24 +215,25 @@
         if j < fan_one:
             hid_sum = hid_sum + act.astype(jnp.float32)
     hid = jnp.concatenate([act, (hid_sum * (1.0 / fan_one)).astype(jnp.bfloat16)], axis=1)
-    logits = dot_nn(hid, w_two) + b_two_ref[...]
+    logits = dot_nt(hid, w_two) + b_two_ref[...]
     shifted = logits - jnp.max(logits, axis=1, keepdims=True)
     log_probs = shifted - jnp.log(jnp.sum(jnp.exp(shifted), axis=1, keepdims=True))
     class_iota = lax.broadcasted_iota(jnp.int32, logits.shape, 1)
     diagonal = lax.broadcasted_iota(jnp.int32, (seeds, seeds), 0) == lax.broadcasted_iota(jnp.int32, (seeds, seeds), 1)
     label = jnp.sum(jnp.where(diagonal, label_ref[...].astype(jnp.float32), 0.0), axis=1, keepdims=True)
     target = (class_iota.astype(jnp.float32) == label).astype(jnp.float32)
-    loss_ref[...] = -jnp.sum(log_probs * target, axis=1, keepdims=True)
+    loss = jnp.sum(log_probs * target, axis=1, keepdims=True)
+    loss_ref[...] = -jnp.sum(jnp.where(diagonal, loss, 0.0), axis=0, keepdims=True)
     d_logits = ((jnp.exp(log_probs) - target) * (1.0 / seeds)).astype(jnp.bfloat16)
-    g_two = dot_tn(hid, d_logits)
-    gb_two = dot_tn(d_logits, jnp.ones((seeds, LANES), jnp.bfloat16))
-    d_hid = dot_nt(d_logits, w_two)
+    g_two = dot_tn(d_logits, hid)
+    gb_two = jnp.sum(d_logits.astype(jnp.float32), axis=0, keepdims=True)
+    d_hid = dot_nn(d_logits, w_two)
     d_hop = d_hid[:, hidden:] * (1.0 / fan_one)
     for j in range(fan_one + 1):
         at = slice(j * seeds, (j + 1) * seeds)
         d_pre = ((d_hop if j < fan_one else d_hid[:, :hidden]) * slope_buf[at, :]).astype(jnp.bfloat16)
         d_buf[at, :] = d_pre
-    gb_one = dot_tn(d_buf[...], jnp.ones((d_buf.shape[0], LANES), jnp.bfloat16))
+    gb_one = dot_nn(jnp.ones((8, d_buf.shape[0]), jnp.bfloat16), d_buf[...])[:1]
     pack_gradients(pack_ref, dot_tn(x_buf[...], d_buf[...]), gb_one, g_two, gb_two)
 
 
@@ -245,7 +247,7 @@
         functools.partial(model_kernel, seeds=seeds, fan_one=fan_one, fan_two=fan_two),
         name="model",
         out_shape=(
-            jax.ShapeDtypeStruct((seeds, 1), jnp.float32),
+            jax.ShapeDtypeStruct((1, seeds), jnp.float32),
             jax.ShapeDtypeStruct((pack_rows, LANES), jnp.float32),
         ),
         in_specs=[pl.BlockSpec(memory_space=pltpu.SMEM)] + [vmem] * 8,
@@ -267,8 +269,8 @@
         self_one,
         neigh_one,
         bias_one.reshape(1, hidden),
-        self_two,
-        neigh_two,
+        self_two.T,
+        neigh_two.T,
         bias_two.reshape(1, classes),
     )
 
@@ -421,57 +423,50 @@
     )(request, features)
 
 
-def pack_plan(feat, hidden):
+def pack_plan(feat, hidden, classes):
     halves = hidden // LANES
     one = 2 * feat * halves
-    low = one + 2 * hidden
-    return halves, one, low, low + hidden
+    high = round_up(classes, 8)
+    tail = one + 2 * halves * high
+    return halves, one, high, tail, tail + 8
 
 
 def pack_gradients(pack_ref, g_one, gb_one, g_two, gb_two):
     hidden, feat = g_one.shape[1], g_one.shape[0] // 2
-    classes = g_two.shape[1]
-    halves, one, low, used = pack_plan(feat, hidden)
+    classes = g_two.shape[0]
+    halves, one, high, tail, used = pack_plan(feat, hidden, classes)
     for h in range(halves):
         pack_ref[h * 2 * feat : (h + 1) * 2 * feat, :] = g_one[:, h * LANES : (h + 1) * LANES]
-    pack_ref[one:low, :] = g_two[:, :LANES]
-    rest = classes - LANES
-    space = LANES // 2 - rest
-    second = jnp.concatenate([gb_two[:, :1], jnp.zeros((hidden - classes, 1), jnp.float32)], axis=0)
-    pack_ref[low:used, :] = jnp.concatenate(
-        [
-            g_two[:hidden, LANES:], gb_one[:, :1], second, jnp.zeros((hidden, space - 2), jnp.float32),
-            g_two[hidden:, LANES:], jnp.zeros((hidden, space), jnp.float32),
-        ],
-        axis=1,
-    )
-    if pack_ref.shape[0] > used:
-        pack_ref[used:, :] = jnp.zeros((pack_ref.shape[0] - used, LANES), jnp.float32)
+    pack_ref[one:, :] = jnp.zeros((pack_ref.shape[0] - one, LANES), jnp.float32)
+    for h in range(2 * halves):
+        pack_ref[one + h * high : one + h * high + classes, :] = g_two[:, h * LANES : (h + 1) * LANES]
+    for h in range(halves):
+        pack_ref[tail + h : tail + h + 1, :] = gb_one[:, h * LANES : (h + 1) * LANES]
+    pack_ref[tail + halves : tail + halves + 1, :] = gb_two[:, :LANES]
+    pack_ref[tail + halves + 1 : tail + halves + 2, : classes - LANES] = gb_two[:, LANES:]
 
 
 def unpack_kernel(pack_ref, self_one, neigh_one, bias_one, self_two, neigh_two, bias_two):
     feat, hidden = self_one.shape
-    classes = self_two.shape[1]
-    rest = classes - LANES
-    halves, one, low, used = pack_plan(feat, hidden)
+    classes = self_two.shape[0]
+    halves, one, high, tail, used = pack_plan(feat, hidden, classes)
     for h in range(halves):
         cols = slice(h * LANES, (h + 1) * LANES)
         at = h * 2 * feat
         self_one[:, cols] = pack_ref[at : at + feat, :]
         neigh_one[:, cols] = pack_ref[at + feat : at + 2 * feat, :]
-    self_two[:, :LANES] = pack_ref[one : one + hidden, :]
-    neigh_two[:, :LANES] = pack_ref[one + hidden : low, :]
-    high = pack_ref[low:used, :]
-    self_two[:, LANES:] = high[:, :rest]
-    neigh_two[:, LANES:] = high[:, LANES // 2 : LANES // 2 + rest]
-    turned = high.T
-    bias_one[...] = turned[rest : rest + 1, :]
-    bias_two[...] = turned[rest + 1 : rest + 2, :classes]
+        at = one + h * high
+        self_two[:, cols] = pack_ref[at : at + classes, :]
+        at = one + (halves + h) * high
+        neigh_two[:, cols] = pack_ref[at : at + classes, :]
+        bias_one[:, cols] = pack_ref[tail + h : tail + h + 1, :]
+    bias_two[:, :LANES] = pack_ref[tail + halves : tail + halves + 1, :]
+    bias_two[:, LANES:] = pack_ref[tail + halves + 1 : tail + halves + 2, : classes - LANES]
 
 
 def unpack(packed, feat, hidden, classes):
     vmem = pl.BlockSpec(memory_space=pltpu.VMEM)
-    shapes = [(feat, hidden), (feat, hidden), (1, hidden), (hidden, classes), (hidden, classes), (1, classes)]
+    shapes = [(feat, hidden), (feat, hidden), (1, hidden), (classes, hidden), (classes, hidden), (1, classes)]
     return pl.pallas_call(
         unpack_kernel,
         name="unpack",
@@ -627,12 +622,13 @@
     stride = HOT_DEV + cap_row
     total = seeds * tree_rows
     id_rows = total // LANES
-    wanted = jnp.concatenate([seed_ids, hop1_ids.reshape(-1), hop2_ids.reshape(-1)])
-    ids = jnp.pad(wanted.reshape(id_rows, LANES), ((0, round_up(id_rows, 8) - id_rows), (0, 0)))
+    spare = round_up(id_rows, 8) * LANES - total
+    wanted = [seed_ids, hop1_ids.reshape(-1), hop2_ids.reshape(-1), jnp.zeros((spare,), jnp.int32)]
+    ids = jnp.concatenate(wanted).reshape(-1, LANES)
     request, addr = plan(ids, partition_map, parts, node_rows, stride, id_rows, cap_pad)
     table = exchange(request, features, cap_row, cap_pad // LANES).reshape(parts * stride, feat)
     hidden, classes = self_two.shape
-    used = pack_plan(feat, hidden)[-1]
+    used = pack_plan(feat, hidden, classes)[-1]
     pack_rows = count * round_up(-(-used // count), 8)
     loss, pieces = model(
         addr.reshape(-1), table, labels, self_one, neigh_one, bias_one, self_two, neigh_two, bias_two,
@@ -641,7 +637,7 @@
     grads = unpack(sum_everywhere(pieces), feat, hidden, classes)
     return (
         loss.reshape(-1), grads[0], grads[1], grads[2].reshape(-1),
-        grads[3], grads[4], grads[5].reshape(-1),
+        grads[3].T, grads[4].T, grads[5].reshape(-1),
     )
 
 

time: 123 us -> 113 us (0.919)
  local copies, waits for them, and re-layouts: 10.5 us -> 3.74 us
  other arithmetic: 1.38 us -> 0 us
    unnamed x6 -> x2, local copies, waits for them, and re-layouts: 8.74 us -> 1.98 us
    pallas_call x1 -> x0, other arithmetic: 1.38 us -> none  [model(): pl.pallas_call(functools.partial(model_kernel, seeds=seeds, fan_one=fan_o...]
where the time goes in v4:
time: 113 us
  Pallas kernels  108 us (96%)
  local copies, waits for them, and re-layouts  3.74 us (3%)
    pallas_call x1, Pallas kernels, exchange(): pl.pallas_call(functools.partial(exchange_kernel, parts=parts, asks=asks)...  47.6 us
    pallas_call x1, Pallas kernels, sum_everywhere(): pl.pallas_call(functools.partial(reduce_kernel, n_dom=n_dom, n_rep=n_rep,...  23.3 us
    pallas_call x1, Pallas kernels, plan(): pl.pallas_call(kernel, name='plan', out_shape=(jax.ShapeDtypeStruct((part...  19.1 us
    pallas_call x1, Pallas kernels, model(): pl.pallas_call(functools.partial(model_kernel, seeds=seeds, fan_one=fan_o...  16.3 us

profile of v4, /device:TPU:0, one launch (start us, length us, event | category | flops | bytes accessed | tf_op | source)
XLA Modules:
  0.0 112.7 jit_solution(5610207046791071382)
XLA Ops:
  0.6 0.8 copy.19
  1.4 0.1 reshape.50
  1.6 1.2 %copy.20 = s32[64,15,10]{2,1,0:T(8,128)S(1)} copy(s32[64,15,10]{0,1,2:T(8,128)} %param.16) | data formatting | bytes 76800 | tf_op args[4]
  2.8 0.3 reshape.51
  3.1 1.3 %concatenate.3 = s32[11264]{0:T(1024)} concatenate(s32[64]{0:T(128)} %param.14, s32[960]{0:T(1024)S(1)} %reshape.50, s32[9600]{0:T(1024)S(1)} %reshape.51, s32[640]{0:T(1024)S(1)} %broadcast_in_dim.3), dimensions={0} | concatenate | bytes 90112 | tf_op jit(solution)/shard_map/concatenate | solution.py:627
  4.4 19.1 %plan.1 = (s32[16,8,128]{2,1,0:T(8,128)}, s32[88,128]{1,0:T(8,128)}) custom-call(s32[88,128]{1,0:T(8,128)} %bitcast.16, s32[1024,128]{1,0:T(8,128)} %bitcast.15), custom_call_target="tpu_custom_call" | custom-call | flops 40000000 | bytes 1000000 | tf_op jit(solution)/shard_map/plan/pallas_call | solution.py:121
  23.5 47.6 %exchange.1 = bf16[16,592,128]{2,1,0:T(8,128)(2,1)} custom-call(s32[16,8,128]{2,1,0:T(8,128)} %get-tuple-element.18.req_ref, bf16[8192,128]{1,0:T(8,128)(2,1)} %feat_ref.1), custom_call_target="tpu_custom_call" | custom-call | tf_op jit(solution)/shard_map/exchange/pallas_call | solution.py:402
  71.1 16.3 %model.1 = (f32[1,64]{1,0:T(1,128)}, f32[1280,128]{1,0:T(8,128)}) custom-call(s32[11264]{0:T(1024)} %bitcast.19, bf16[9472,128]{1,0:T(8,128)(2,1)} %bitcast.14, s32[1,64]{1,0:T(1,128)} %bitcast.22, bf16[128,256]{1,0:T(8,128)(2,1)} %self_one.1, bf16[128,256]{1,0:T(8,128)(2,1)} %neigh_one.1, f32[1,256]{1,0:T(1,128)} %bitcast.20, bf16[172,256]{1,0:T(8,128)(2,1)} %bitcast.17, ...), custom_call_target="tpu_custom_call" | custom-call | flops 100000000 | bytes 4000000 | tf_op jit(solution)/shard_map/model/pallas_call | solution.py:246
  87.4 23.3 %sum_everywhere.1.pack_ref = f32[1280,128]{1,0:T(8,128)} custom-call(f32[1280,128]{1,0:T(8,128)} %get-tuple-element.20.part_ref), custom_call_target="tpu_custom_call" | custom-call | tf_op jit(solution)/shard_map/sum_everywhere/pallas_call | solution.py:590
  110.8 1.9 %unpack.1 = (f32[128,256]{1,0:T(8,128)}, f32[128,256]{1,0:T(8,128)}, f32[1,256]{1,0:T(1,128)}, f32[172,256]{1,0:T(8,128)}, f32[172,256]{1,0:T(8,128)}, /*index=5*/f32[1,172]{1,0:T(1,128)}) custom-call(f32[1280,128]{1,0:T(8,128)} %sum_everywhere.1.pack_ref), custom_call_target="tpu_custom_call" | custom-call | tf_op jit(solution)/shard_map/unpack/pallas_call | solution.py:470
  (1 shorter events, 0.0 us)

commit v5 on v4

--- a/solution.py
+++ b/solution.py
@@ -377,7 +377,7 @@
 
     served = 1
     for level in range(1, bits):
-        until = parts * level // bits
+        until = max(1, parts * (level - 1) // bits)
         lax.fori_loop(served, until, serve, 0)
         served = until
         shared(level - 1).wait_recv()

time: 113 us -> 113 us (level)
  no operation moved by 1% of the time
where the time goes in v5:
time: 113 us; the launch traced here: 112 us
  Pallas kernels  108 us (96%)
  local copies, waits for them, and re-layouts  3.74 us (3%)
    pallas_call x1, Pallas kernels, exchange(): pl.pallas_call(functools.partial(exchange_kernel, parts=parts, asks=asks)...  46.6 us
    pallas_call x1, Pallas kernels, sum_everywhere(): pl.pallas_call(functools.partial(reduce_kernel, n_dom=n_dom, n_rep=n_rep,...  24.1 us
    pallas_call x1, Pallas kernels, plan(): pl.pallas_call(kernel, name='plan', out_shape=(jax.ShapeDtypeStruct((part...  19.1 us
    pallas_call x1, Pallas kernels, model(): pl.pallas_call(functools.partial(model_kernel, seeds=seeds, fan_one=fan_o...  16.3 us

profile of v5, /device:TPU:0, one launch (start us, length us, event | category | flops | bytes accessed | tf_op | source)
XLA Modules:
  0.0 112.5 jit_solution(7829606625085389448)
XLA Ops:
  0.6 0.8 copy.19
  1.4 0.1 reshape.50
  1.6 1.2 %copy.20 = s32[64,15,10]{2,1,0:T(8,128)S(1)} copy(s32[64,15,10]{0,1,2:T(8,128)} %param.16) | data formatting | bytes 76800 | tf_op args[4]
  2.8 0.3 reshape.51
  3.1 1.3 %concatenate.3 = s32[11264]{0:T(1024)} concatenate(s32[64]{0:T(128)} %param.14, s32[960]{0:T(1024)S(1)} %reshape.50, s32[9600]{0:T(1024)S(1)} %reshape.51, s32[640]{0:T(1024)S(1)} %broadcast_in_dim.3), dimensions={0} | concatenate | bytes 90112 | tf_op jit(solution)/shard_map/concatenate | solution.py:627
  4.4 19.1 %plan.1 = (s32[16,8,128]{2,1,0:T(8,128)}, s32[88,128]{1,0:T(8,128)}) custom-call(s32[88,128]{1,0:T(8,128)} %bitcast.16, s32[1024,128]{1,0:T(8,128)} %bitcast.15), custom_call_target="tpu_custom_call" | custom-call | flops 40000000 | bytes 1000000 | tf_op jit(solution)/shard_map/plan/pallas_call | solution.py:121
  23.5 46.6 %exchange.1 = bf16[16,592,128]{2,1,0:T(8,128)(2,1)} custom-call(s32[16,8,128]{2,1,0:T(8,128)} %get-tuple-element.18.req_ref, bf16[8192,128]{1,0:T(8,128)(2,1)} %feat_ref.1), custom_call_target="tpu_custom_call" | custom-call | tf_op jit(solution)/shard_map/exchange/pallas_call | solution.py:402
  70.1 16.3 %model.1 = (f32[1,64]{1,0:T(1,128)}, f32[1280,128]{1,0:T(8,128)}) custom-call(s32[11264]{0:T(1024)} %bitcast.19, bf16[9472,128]{1,0:T(8,128)(2,1)} %bitcast.14, s32[1,64]{1,0:T(1,128)} %bitcast.22, bf16[128,256]{1,0:T(8,128)(2,1)} %self_one.1, bf16[128,256]{1,0:T(8,128)(2,1)} %neigh_one.1, f32[1,256]{1,0:T(1,128)} %bitcast.20, bf16[172,256]{1,0:T(8,128)(2,1)} %bitcast.17, ...), custom_call_target="tpu_custom_call" | custom-call | flops 100000000 | bytes 4000000 | tf_op jit(solution)/shard_map/model/pallas_call | solution.py:246
  86.4 24.1 %sum_everywhere.1.pack_ref = f32[1280,128]{1,0:T(8,128)} custom-call(f32[1280,128]{1,0:T(8,128)} %get-tuple-element.20.part_ref), custom_call_target="tpu_custom_call" | custom-call | tf_op jit(solution)/shard_map/sum_everywhere/pallas_call | solution.py:590
  110.6 1.9 %unpack.1 = (f32[128,256]{1,0:T(8,128)}, f32[128,256]{1,0:T(8,128)}, f32[1,256]{1,0:T(1,128)}, f32[172,256]{1,0:T(8,128)}, f32[172,256]{1,0:T(8,128)}, /*index=5*/f32[1,172]{1,0:T(1,128)}) custom-call(f32[1280,128]{1,0:T(8,128)} %sum_everywhere.1.pack_ref), custom_call_target="tpu_custom_call" | custom-call | tf_op jit(solution)/shard_map/unpack/pallas_call | solution.py:470
  (1 shorter events, 0.0 us)
